TPU v7x, 32 devices: a 4x4x1 block of a 4x4x8 slice. The times are simulated.
32 devices in a mesh: data: 1 (over z), expert: 32 (over y, x, core).
Axes of the slice: x: 4, y: 4, z: 1, core: 2. Of those that a mesh axis runs over, the one named last changes fastest.
The devices are a block of a 4x4x8 slice.
Arguments:
- x: bfloat16 [24576, 2048], P(('data', 'expert'))
- idx: int32 [24576, 7], P(('data', 'expert'))
- g: float32 [24576, 7], P(('data', 'expert'))
- hot_tok: int32 [12288], P(('data', 'expert'))
- hot_g: float32 [12288], P(('data', 'expert'))
- ln1: float32 [2048], replicated
- wq: bfloat16 [2048, 16, 128], replicated
- wk: bfloat16 [2048, 16, 128], replicated
- wv: bfloat16 [2048, 16, 128], replicated
- wo: bfloat16 [16, 128, 2048], replicated
- ln2: float32 [2048], replicated
- w1: bfloat16 [64, 2048, 1024], P('expert')
- w3: bfloat16 [64, 2048, 1024], P('expert')
- w2: bfloat16 [64, 1024, 2048], P('expert')
Outputs:
- output: bfloat16 [24576, 2048], P(('data', 'expert'))
All inputs are finite; a program needn't handle non-finite values.
Results may differ from a plain program's by a relative error of at most 0.0105547.
Values are sent between devices in bfloat16 or wider.
A program may use at most 768 MiB of HBM per device.

v0:
```python
import jax
import jax.numpy as jnp
from jax import lax
from jax.sharding import PartitionSpec as P

EPS = 1e-6
ROPE_BASE = 10000.0
HOT_ID = 1
F32 = jnp.float32
BF16 = jnp.bfloat16


def _rms(v, w):
    v = v.astype(F32)
    return (v * lax.rsqrt(jnp.mean(v * v, axis=-1, keepdims=True) + EPS) * w).astype(BF16)


def _rope(t):
    n_tok, _, dh = t.shape
    half = dh // 2
    freq = ROPE_BASE ** (-jnp.arange(half, dtype=F32) / half)
    ang = jnp.arange(n_tok, dtype=F32)[:, None] * freq[None, :]
    cos = jnp.cos(ang)[:, None, :]
    sin = jnp.sin(ang)[:, None, :]
    t1, t2 = t[..., :half], t[..., half:]
    return jnp.concatenate([t1 * cos - t2 * sin, t2 * cos + t1 * sin], axis=-1)


def _attention(x, ln1, wq, wk, wv, wo):
    n_tok = x.shape[0]
    dh = wq.shape[2]
    a = _rms(x, ln1)
    q = _rope(jnp.einsum('td,dhk->thk', a, wq, preferred_element_type=F32)).astype(BF16)
    k = _rope(jnp.einsum('td,dhk->thk', a, wk, preferred_element_type=F32)).astype(BF16)
    v = jnp.einsum('td,dhk->thk', a, wv, preferred_element_type=F32).astype(BF16)
    s = jnp.einsum('qhk,shk->hqs', q, k, preferred_element_type=F32) * dh ** -0.5
    mask = jnp.tril(jnp.ones((n_tok, n_tok), bool))
    p = jax.nn.softmax(jnp.where(mask[None], s, -jnp.inf), axis=-1).astype(BF16)
    o = jnp.einsum('hqs,shk->qhk', p, v, preferred_element_type=F32).astype(BF16)
    out = jnp.einsum('qhk,hkd->qd', o, wo, preferred_element_type=F32)
    return (x.astype(F32) + out).astype(BF16)


def _capacity(t, kc, n_exp):
    c0 = (t * kc + n_exp - 2) // (n_exp - 1)
    return 8 * ((3 * c0 + 15) // 16)


def _slots(e, n_exp, cap):
    r = e.shape[0]
    order = jnp.argsort(e, stable=True)
    counts = jnp.zeros((n_exp,), jnp.int32).at[e].add(1)
    starts = jnp.cumsum(counts) - counts
    rank = jnp.zeros((r,), jnp.int32).at[order].set(jnp.arange(r, dtype=jnp.int32) - starts[e[order]])
    return e * cap + rank


def _ffn(a, w1, w3, w2):
    h1 = jnp.dot(a, w1, preferred_element_type=F32)
    h3 = jnp.dot(a, w3, preferred_element_type=F32)
    z = (jax.nn.silu(h1) * h3).astype(BF16)
    return jnp.dot(z, w2, preferred_element_type=F32).astype(BF16)


def _experts(a, w1, w3, w2):
    h1 = jnp.einsum('erd,edf->erf', a, w1, preferred_element_type=F32)
    h3 = jnp.einsum('erd,edf->erf', a, w3, preferred_element_type=F32)
    z = (jax.nn.silu(h1) * h3).astype(BF16)
    return jnp.einsum('erf,efd->erd', z, w2, preferred_element_type=F32).astype(BF16)


def _combine(rows, g, hot_tok, hot_g, hot_out):
    t, kc = g.shape
    y = jnp.sum(g[:, :, None] * rows.reshape(t, kc, -1).astype(F32), axis=1)
    y = y.at[hot_tok].add(hot_g[:, None] * hot_out.astype(F32))
    return y.astype(BF16)


def solution(mesh):
    n = mesh.shape['expert']

    def local(x, idx, g, hot_tok, hot_g, ln1, wq, wk, wv, wo, ln2, w1, w3, w2):
        T, D = x.shape
        KC = idx.shape[1]
        el = w1.shape[0]
        E = el * n
        C = _capacity(T, KC, E)
        ch = hot_tok.shape[0]
        owner = HOT_ID // el
        lh = HOT_ID % el
        me = lax.axis_index('expert')
        u = _rms(_attention(x, ln1, wq, wk, wv, wo), ln2)
        slot = _slots(idx.reshape(-1), E, C)
        tok = jnp.arange(T * KC) // KC
        buf = jnp.zeros((E * C, D), BF16).at[slot].set(u[tok])
        recv = lax.all_to_all(buf, 'expert', 0, 0, tiled=True)
        xin = recv.reshape(n, el, C, D).transpose(1, 0, 2, 3).reshape(el, n * C, D)
        out = _experts(xin, w1, w3, w2)
        out = out.reshape(el, n, C, D).transpose(1, 0, 2, 3).reshape(E * C, D)
        back = lax.all_to_all(out, 'expert', 0, 0, tiled=True)
        rows = back[slot]
        hrows = lax.all_gather(u[hot_tok], 'expert', tiled=True)
        hout = lax.cond(me == owner,
                        lambda r: _ffn(r, w1[lh], w3[lh], w2[lh]),
                        lambda r: jnp.zeros_like(r),
                        hrows)
        hback = lax.all_to_all(hout, 'expert', 0, 0, tiled=True)
        hot_out = hback.reshape(n, ch, D)[owner]
        return _combine(rows, g, hot_tok, hot_g, hot_out)

    tk = ('data', 'expert')
    rep3 = P(None, None, None)
    exp3 = P('expert', None, None)
    return jax.shard_map(
        local, mesh=mesh,
        in_specs=(P(tk, None), P(tk, None), P(tk, None), P(tk), P(tk), P(None),
                  rep3, rep3, rep3, rep3, P(None), exp3, exp3, exp3),
        out_specs=P(tk, None), check_vma=False)
```

profile of v0, /device:TPU:107, one launch (start us, length us, event | category | flops | bytes accessed | tf_op | source)
XLA Modules:
  0.0 2242.0 jit_solution(7003962186709760780)
XLA Ops:
  26.7 12.6 copy.25
  50.2 12.4 copy.26
  76.0 19.3 fusion.69
  95.3 28.5 %fusion.26 = (f32[768]{0:T(1024)S(1)}, bf16[768,2048]{1,0:T(8,128)(2,1)}) fusion(bf16[16,128,2048]{2,1,0:T(8,128)(2,1)} %param.25, f32[16,768,768]{1,2,0:T(8,128)} %get-tuple-element.156, f32[16,768]{1,0:T(8,128)S(1)} %get-tuple-element.155, bf16[768,16,128]{2,1,0:T(8,128)(2,1)} %copy.45, bf16[768,2048]{1,0:T(8,128)(2,1)S(1)} %copy-done.2), kind=kOutput, calls=%fused_computation.42 | convolution fusion | flops 8888253440 | bytes 55626752 | tf_op jit(solution)/shard_map/qhk,hkd->qd/dot_general | solution.py:40
  140.5 28.0 %gather_fusion = s32[5376]{0:T(1024)S(1)} fusion(s32[5376]{0:T(1024)S(1)} %reshape.211, s32[6144]{0:T(1024)S(1)} %pad_clamp_fusion.3), kind=kCustom, calls=%fused_computation | custom fusion | bytes 64512 | tf_op jit(solution)/shard_map/gather | solution.py:54
  168.6 37.6 %scatter_custom_fusion = s32[64]{0:T(128)S(1)} fusion(s32[5376]{0:T(1024)S(1)} %fusion.47, s32[5376]{0:T(1024)S(1)} %broadcast.316, s32[]{:T(128)} %constant.13.clone.1), kind=kCustom, calls=%fused_computation.157 | custom fusion | flops 5376 | bytes 260 | tf_op jit(solution)/shard_map/scatter-add | solution.py:52
  217.6 36.1 %select_subtract_fusion = s32[5376]{0:T(1024)S(1)} fusion(pred[5376]{0:T(1024)(128)(4,1)S(1)} %get-tuple-element.80, pred[5376]{0:T(1024)(128)(4,1)S(1)} %get-tuple-element.79, pred[5376]{0:T(1024)(128)(4,1)S(1)} %get-tuple-element.78, pred[5376]{0:T(1024)(128)(4,1)S(1)} %get-tuple-element.77, pred[5376]{0:T(1024)(128)(4,1)S(1)} %get-tuple-element.76, ...), kind=kLoop, calls=%fused_computation.145 | loop fusion | flops 311808 | bytes 349668 | tf_op jit(solution)/shard_map/sub | solution.py:54
  253.7 20.2 scatter_custom_fusion.1
  274.1 21.5 gather_fusion.1
  301.7 123.9 %scatter_custom_fusion.2 = bf16[8704,2048]{1,0:T(8,128)(2,1)} fusion(s32[5376]{0:T(1024)S(1)} %get-tuple-element.22, bf16[5376,2048]{1,0:T(8,128)(2,1)} %gather_fusion.1, s32[6144]{0:T(1024)S(1)} %pad_clamp_fusion.1, bf16[]{:T(256)} %constant.23.clone.1), kind=kCustom, calls=%fused_computation.27 | custom fusion | bytes 35652096 | tf_op jit(solution)/shard_map/scatter | solution.py:95
  425.6 437.5 %all_to_all.30 = bf16[32,272,2048]{2,1,0:T(8,128)(2,1)} all-to-all(bf16[32,272,2048]{2,1,0:T(8,128)(2,1)} %bitcast.143), channel_id=1, replica_groups=mesh['data'=1,'expert'=32] {'expert'}, dimensions={0} | all-to-all | bytes 71303168 | tf_op jit(solution)/shard_map/all_to_all | solution.py:96
  863.1 24.0 %copy.29 = bf16[2,32,136,2048]{3,2,1,0:T(8,128)(2,1)} copy(bf16[2,32,136,2048]{3,2,0,1:T(8,128)(2,1)} %bitcast.144) | data formatting | bytes 71303168 | tf_op jit(solution)/shard_map/transpose | solution.py:97
  887.1 45.9 %fusion.72 = f32[2,4352,1024]{2,1,0:T(8,128)} fusion(bf16[2,4352,2048]{2,1,0:T(8,128)(2,1)} %bitcast.145, bf16[2,2048,1024]{2,1,0:T(8,128)(2,1)} %param.27), kind=kOutput, calls=%fused_computation.170 | convolution fusion | flops 36507222016 | bytes 79691776 | tf_op jit(solution)/shard_map/erd,edf->erf/dot_general | solution.py:66
  933.0 49.4 %multiply_convert_fusion.1.clone.4 = bf16[2,4352,1024]{2,1,0:T(8,128)(2,1)} fusion(f32[2,4352,1024]{2,1,0:T(8,128)} %fusion.72, bf16[2,4352,2048]{2,1,0:T(8,128)(2,1)} %bitcast.146, bf16[2,2048,1024]{2,1,0:T(8,128)(2,1)} %param.28), kind=kOutput, calls=%fused_computation.24.clone.clone.clone.1 | convolution fusion | flops 36560699392 | bytes 97517568 | tf_op jit(solution)/shard_map/erd,edf->erf/dot_general | solution.py:67
  982.5 46.3 %convolution_convert_fusion.1 = bf16[2,4352,2048]{2,1,0:T(8,128)(2,1)} fusion(bf16[2,1024,2048]{2,1,0:T(8,128)(2,1)} %param.29, bf16[2,4352,1024]{2,1,0:T(8,128)(2,1)} %multiply_convert_fusion.1.clone.4), kind=kOutput, calls=%fused_computation.26 | convolution fusion | flops 36525047808 | bytes 61865984 | tf_op jit(solution)/shard_map/erf,efd->erd/dot_general | solution.py:69
  1028.8 24.1 %copy.30 = bf16[2,32,136,2048]{3,2,0,1:T(8,128)(2,1)} copy(bf16[2,32,136,2048]{3,2,1,0:T(8,128)(2,1)} %bitcast.147) | data formatting | bytes 71303168 | tf_op jit(solution)/shard_map/reshape | solution.py:99
  1059.3 23.7 %conditional.1 = (bf16[12288,2048]{1,0:T(8,128)(2,1)}) conditional(s32[]{:T(128)} %convert_element_type.73, () %tuple.11, (bf16[2,2048,1024]{2,1,0:T(8,128)(2,1)}, bf16[12288,2048]{1,0:T(8,128)(2,1)}, bf16[2,2048,1024]{2,1,0:T(8,128)(2,1)}, bf16[2,1024,2048]{2,1,0:T(8,128)(2,1)}) %tuple.12), branch_computations={%region_10.11_spmd, %region_11.12_spmd} | conditional | flops 154719485952 | bytes 314572800 | solution.py:103
  1059.3 16.1 broadcast.162
  1082.9 458.7 %all-to-all-done.1 = bf16[32,272,2048]{2,1,0:T(8,128)(2,1)} async-done(((bf16[32,272,2048]{2,1,0:T(8,128)(2,1)}), bf16[32,272,2048]{2,1,0:T(8,128)(2,1)}, u32[]{:S(2)}, u32[]{:S(2)}) %all-to-all-start.1) | async-done | bytes 35651616 | tf_op jit(solution)/shard_map/all_to_all | solution.py:100
  1546.9 54.5 %gather_fusion.2 = bf16[5376,2048]{1,0:T(8,128)(2,1)} fusion(bf16[8704,2048]{1,0:T(8,128)(2,1)} %bitcast.82, s32[6144]{0:T(1024)S(1)} %pad_clamp_fusion), kind=kCustom, calls=%fused_computation.2 | custom fusion | bytes 44061696 | tf_op jit(solution)/shard_map/gather | solution.py:101
  1601.4 30.9 %reshape.218 = f32[768,7,2048]{2,1,0:T(8,128)} reshape(bf16[5376,2048]{1,0:T(8,128)(2,1)} %gather_fusion.2) | data formatting | bytes 66060288 | tf_op jit(solution)/shard_map/convert_element_type | solution.py:74
  1632.3 23.4 %multiply_reduce_fusion = f32[768,2048]{1,0:T(8,128)} fusion(f32[768,7,2048]{2,1,0:T(8,128)} %reshape.218, f32[768,7]{1,0:T(8,128)S(1)} %copy.21), kind=kLoop, calls=%fused_computation.20 | loop fusion | flops 20447232 | bytes 50353152 | tf_op jit(solution)/shard_map/reduce_sum | solution.py:74
  1655.7 562.6 %all-to-all-done.2 = bf16[32,384,2048]{2,1,0:T(8,128)(2,1)} async-done(((bf16[32,384,2048]{2,1,0:T(8,128)(2,1)}), bf16[32,384,2048]{2,1,0:T(8,128)(2,1)}, u32[]{:S(2)}, u32[]{:S(2)}) %all-to-all-start.2) | async-done | bytes 50331680 | tf_op jit(solution)/shard_map/all_to_all | solution.py:107
  2218.3 11.7 scatter_custom_fusion.3
  (72 shorter events, 95.3 us)
Async XLA Ops:
  6.5 1052.7 %all-gather.3.cloned.1.call-start = ((), (), s32[]{:S(2)}) async-start(), calls=%async_computation.3 | async-start | bytes 51904512 | tf_op jit(solution)/shard_map/all_gather | solution.py:102
  8.2 0.6 copy-start.9
  26.7 12.6 copy-start.2
  26.7 12.6 copy-start.11
  62.6 9.4 copy-start
  95.3 28.5 %copy-start.8 = (f32[2048]{0:T(1024)S(1)}, f32[2048]{0:T(1024)}, u32[]{:S(2)}) copy-start(f32[2048]{0:T(1024)} %param.26) | copy-start | bytes 24580
  123.7 2.7 copy-start.7
  130.7 0.8 copy-start.1
  140.5 28.0 %copy-start.5 = (s32[5376,1]{0,1:T(1,128)S(1)}, s32[5376,1]{0,1:T(1,128)}, u32[]{:S(2)}) copy-start(s32[5376,1]{0,1:T(1,128)} %reshape.212) | copy-start | bytes 64516
  295.7 130.0 %copy-start.3 = (s32[5376]{0:T(1024)}, s32[5376]{0:T(1024)S(1)}, u32[]{:S(2)}) copy-start(s32[5376]{0:T(1024)S(1)} %compare_select_fusion.9) | copy-start | bytes 64516
  1052.9 488.8 %all-to-all-start.1 = ((bf16[32,272,2048]{2,1,0:T(8,128)(2,1)}), bf16[32,272,2048]{2,1,0:T(8,128)(2,1)}, u32[]{:S(2)}, u32[]{:S(2)}) async-start(bf16[32,272,2048]{2,1,0:T(8,128)(2,1)} %bitcast.142), calls=%async_computation.1 | async-start | bytes 71303168 | tf_op jit(solution)/shard_map/all_to_all | solution.py:100
  1541.7 5.0 copy-start.6
  1541.7 5.2 copy-start.4
  1541.7 676.6 %all-to-all-start.2 = ((bf16[32,384,2048]{2,1,0:T(8,128)(2,1)}), bf16[32,384,2048]{2,1,0:T(8,128)(2,1)}, u32[]{:S(2)}, u32[]{:S(2)}) async-start(bf16[32,384,2048]{2,1,0:T(8,128)(2,1)} %bitcast.141), calls=%async_computation.2 | async-start | bytes 100663296 | tf_op jit(solution)/shard_map/all_to_all | solution.py:107
  1632.3 586.0 %copy-start.10 = (f32[384]{0:T(512)S(1)}, f32[384]{0:T(512)}, u32[]{:S(2)}) copy-start(f32[384]{0:T(512)} %param.20) | copy-start | bytes 4612
Sparse Core Ops, SparseCore 0:
  129.9 153.1 all-gather.2
where the time goes:
time: 2250 us; the launch traced here: 2240 us
  waiting for transfers between devices  1020 us (45%)
  blocking collectives  437 us (19%)
  local copies, waits for them, and re-layouts  383 us (17%)
  matrix products  220 us (10%)
  other arithmetic  147 us (7%)
    all_to_all x1, waiting for transfers between devices, local(): hback = lax.all_to_all(hout, 'expert', 0, 0, tiled=True)  563 us
    all_to_all x1, waiting for transfers between devices, local(): back = lax.all_to_all(out, 'expert', 0, 0, tiled=True)  459 us
    all_to_all x1, blocking collectives, local(): recv = lax.all_to_all(buf, 'expert', 0, 0, tiled=True)  437 us
    scatter x2, local copies, waits for them, and re-layouts, local(): buf = jnp.zeros((E * C, D), BF16).at[slot].set(u[tok])  124 us
    gather x1, local copies, waits for them, and re-layouts, local(): rows = back[slot]  54.5 us
    dot_general x1, matrix products, _experts(): h3 = jnp.einsum('erd,edf->erf', a, w3, preferred_element_type=F32)  49.4 us
    dot_general x1, matrix products, _experts(): jnp.einsum('erf,efd->erd', z, w2, preferred_element_type=F32).astype(BF16)  46.3 us
    dot_general x1, matrix products, _experts(): h1 = jnp.einsum('erd,edf->erf', a, w1, preferred_element_type=F32)  45.9 us
  transfers between devices with their start and end apart: 3, of which 2 were waited for; matrix products, arithmetic and copies ran while one was open for 27% of the time, Pallas kernels for 0%

commit v1 on v0

v1 whole, which is shorter than its diff:
```python
import jax
import jax.numpy as jnp
from jax import lax
from jax.sharding import PartitionSpec as P

EPS = 1e-6
ROPE_BASE = 10000.0
HOT_ID = 1
CHUNKS = 2
F32 = jnp.float32
BF16 = jnp.bfloat16


def _rms(v, w):
    v = v.astype(F32)
    return (v * lax.rsqrt(jnp.mean(v * v, axis=-1, keepdims=True) + EPS) * w).astype(BF16)


def _rope(t, start):
    n_tok, _, dh = t.shape
    half = dh // 2
    freq = ROPE_BASE ** (-jnp.arange(half, dtype=F32) / half)
    ang = (start + jnp.arange(n_tok, dtype=F32))[:, None] * freq[None, :]
    cos = jnp.cos(ang)[:, None, :]
    sin = jnp.sin(ang)[:, None, :]
    t1, t2 = t[..., :half], t[..., half:]
    return jnp.concatenate([t1 * cos - t2 * sin, t2 * cos + t1 * sin], axis=-1)


def _attention_chunks(x, ln1, wq, wk, wv, wo, chunks):
    n_tok = x.shape[0]
    dh = wq.shape[2]
    step = n_tok // chunks
    ks, vs = [], []
    before = None
    for c in range(chunks):
        lo = c * step
        xc = x[lo:lo + step]
        if before is not None:
            xc, _ = lax.optimization_barrier((xc, before))
        a = _rms(xc, ln1)
        q = _rope(jnp.einsum('td,dhk->thk', a, wq, preferred_element_type=F32), lo).astype(BF16)
        ks.append(_rope(jnp.einsum('td,dhk->thk', a, wk, preferred_element_type=F32), lo).astype(BF16))
        vs.append(jnp.einsum('td,dhk->thk', a, wv, preferred_element_type=F32).astype(BF16))
        k = jnp.concatenate(ks, axis=0)
        v = jnp.concatenate(vs, axis=0)
        s = jnp.einsum('qhk,shk->hqs', q, k, preferred_element_type=F32) * dh ** -0.5
        mask = (lo + jnp.arange(step))[:, None] >= jnp.arange(lo + step)[None, :]
        p = jax.nn.softmax(jnp.where(mask[None], s, -jnp.inf), axis=-1).astype(BF16)
        o = jnp.einsum('hqs,shk->qhk', p, v, preferred_element_type=F32).astype(BF16)
        out = jnp.einsum('qhk,hkd->qd', o, wo, preferred_element_type=F32)
        before = yield (xc.astype(F32) + out).astype(BF16)


def _capacity(t, kc, n_exp):
    c0 = (t * kc + n_exp - 2) // (n_exp - 1)
    return 8 * ((3 * c0 + 15) // 16)


def _ffn(a, w1, w3, w2):
    h1 = jnp.dot(a, w1, preferred_element_type=F32)
    h3 = jnp.dot(a, w3, preferred_element_type=F32)
    z = (jax.nn.silu(h1) * h3).astype(BF16)
    return jnp.dot(z, w2, preferred_element_type=F32).astype(BF16)


def _parts(g):
    hi = lax.reduce_precision(g, 8, 7)
    mid = lax.reduce_precision(g - hi, 8, 7)
    low = g - hi - mid
    return [v.astype(BF16) for v in (hi, mid, low)]


def _gated(g_parts, hit, rows):
    lhs = jnp.concatenate([jnp.where(hit, v, jnp.zeros((), BF16)) for v in g_parts], axis=0)
    out = jnp.dot(lhs, rows, preferred_element_type=F32)
    return jnp.sum(out.reshape(len(g_parts), -1, out.shape[-1]), axis=0)


def solution(mesh):
    n = mesh.shape['expert']

    def local(x, idx, g, hot_tok, hot_g, ln1, wq, wk, wv, wo, ln2, w1, w3, w2):
        T, D = x.shape
        KC = idx.shape[1]
        el = w1.shape[0]
        E = el * n
        C = _capacity(T, KC, E)
        owner = HOT_ID // el
        lh = HOT_ID % el
        me = lax.axis_index('expert')

        own = me == owner
        hw = [lax.psum(jnp.where(own, w[lh], jnp.zeros((), BF16)), 'expert') for w in (w1, w3, w2)]

        same = idx[:, :, None] == jnp.arange(E, dtype=jnp.int32)
        has = jnp.any(same, axis=1)
        gate = jnp.sum(jnp.where(same, g[:, :, None], 0.0), axis=1)
        tri = jnp.tril(jnp.ones((T, T), BF16))
        upto = jnp.dot(tri, has.astype(BF16), preferred_element_type=F32)
        place = jnp.where(has, upto.astype(jnp.int32) - 1, -1)
        theirs = lax.all_to_all(place.T, 'expert', 0, 0, tiled=True).reshape(n, el, T)

        step = T // CHUNKS
        us = []
        xin = [None] * el
        slot = jnp.arange(C, dtype=jnp.int32)
        chunks = _attention_chunks(x, ln1, wq, wk, wv, wo, CHUNKS)
        u = None
        for c in range(CHUNKS):
            u = _rms(chunks.send(u), ln2)
            if c == 0:
                u, *hw = lax.optimization_barrier((u, *hw))
            us.append(u)
            every = lax.all_gather(u, 'expert')
            for l in range(el):
                pick = (theirs[:, l, None, c * step:(c + 1) * step] == slot[:, None]).astype(BF16)
                part = jnp.einsum('srt,std->srd', pick, every, preferred_element_type=F32).astype(BF16)
                xin[l] = part if xin[l] is None else xin[l] + part
        u = jnp.concatenate(us, axis=0)

        y = jnp.zeros((T, D), F32)
        hot_hit = hot_tok[:, None] == jnp.arange(T, dtype=jnp.int32)
        hot_rows = jnp.dot(hot_hit.astype(BF16), u, preferred_element_type=F32).astype(BF16)
        hot_out = _ffn(hot_rows, *hw)
        y = y + _gated([v[None, :] for v in _parts(hot_g)], hot_hit.T, hot_out)

        g_parts = _parts(gate)
        for l in range(el):
            out = _ffn(xin[l].reshape(n * C, D), w1[l], w3[l], w2[l])
            back = lax.all_to_all(out, 'expert', 0, 0, tiled=True)
            hit = (place.reshape(T, n, el)[:, :, l, None] == slot).reshape(T, n * C)
            gl = [jnp.broadcast_to(v.reshape(T, n, el)[:, :, l, None], (T, n, C)).reshape(T, n * C)
                  for v in g_parts]
            y = y + _gated(gl, hit, back)
        return y.astype(BF16)

    tk = ('data', 'expert')
    rep3 = P(None, None, None)
    exp3 = P('expert', None, None)
    return jax.shard_map(
        local, mesh=mesh,
        in_specs=(P(tk, None), P(tk, None), P(tk, None), P(tk), P(tk), P(None),
                  rep3, rep3, rep3, rep3, P(None), exp3, exp3, exp3),
        out_specs=P(tk, None), check_vma=False)
```

time: 2250 us -> 1120 us (0.50)
  waiting for transfers between devices: 1020 us -> 424 us
  blocking collectives: 437 us -> 14.8 us
  local copies, waits for them, and re-layouts: 383 us -> 82.7 us
  matrix products: 220 us -> 458 us
  other arithmetic: 147 us -> 106 us
    all_to_all x1 -> x0, waiting for transfers between devices: 563 us -> none  [local(): hback = lax.all_to_all(hout, 'expert', 0, 0, tiled=True)]
    all_to_all x1, blocking collectives: 437 us -> 14.8 us  [local(): lax.all_to_all(place.T, 'expert', 0, 0, tiled=True).reshape(n, el, T)]
    all_to_all x1 -> x2, waiting for transfers between devices: 459 us -> 171 us  [local(): back = lax.all_to_all(out, 'expert', 0, 0, tiled=True)]
    dot_general x5 -> x23, matrix products: 180 us -> 434 us  [the longest x3 115 us: _gated(): out = jnp.dot(lhs, rows, preferred_element_type=F32)]
    all_gather x1 -> x2, waiting for transfers between devices: 0.02 us -> 200 us  [local(): every = lax.all_gather(u, 'expert')]
    scatter x3 -> x0, local copies, waits for them, and re-layouts: 144 us -> none  [the longest x2 124 us: local(): buf = jnp.zeros((E * C, D), BF16).at[slot].set(u[tok])]
    gather x8 -> x0, local copies, waits for them, and re-layouts: 110 us -> none  [the longest x1 54.5 us: local(): rows = back[slot]]
    psum x0 -> x1, waiting for transfers between devices: none -> 53.7 us  [local(): lax.psum(jnp.where(own, w[lh], jnp.zeros((), BF16)), 'expert')]
  transfers between devices with their start and end apart: 3 -> 5, of which waited for: 2 -> 5; matrix products, arithmetic and copies ran while one was open for 27% -> 42% of each run, Pallas kernels for 0% -> 0%
where the time goes in v1:
time: 1120 us; the launch traced here: 1110 us
  matrix products  458 us (41%)
  waiting for transfers between devices  424 us (38%)
  other arithmetic  106 us (9%)
  local copies, waits for them, and re-layouts  82.7 us (7%)
  blocking collectives  14.8 us (1%)
  between operations  14.2 us (1%)
  starting transfers between devices  11.4 us (1%)
    all_gather x2, waiting for transfers between devices, local(): every = lax.all_gather(u, 'expert')  200 us
    all_to_all x2, waiting for transfers between devices, local(): back = lax.all_to_all(out, 'expert', 0, 0, tiled=True)  171 us
    dot_general x3, matrix products, _gated(): out = jnp.dot(lhs, rows, preferred_element_type=F32)  115 us
    dot_general x4, matrix products, local(): jnp.einsum('srt,std->srd', pick, every, preferred_element_type=F32)  106 us
    dot_general x3, matrix products, _ffn(): h3 = jnp.dot(a, w3, preferred_element_type=F32)  59.7 us
    psum x1, waiting for transfers between devices, local(): lax.psum(jnp.where(own, w[lh], jnp.zeros((), BF16)), 'expert')  53.7 us
    dot_general x3, matrix products, _ffn(): h1 = jnp.dot(a, w1, preferred_element_type=F32)  51.7 us
    dot_general x2, matrix products, _ffn(): return jnp.dot(z, w2, preferred_element_type=F32).astype(BF16)  50.2 us
  transfers between devices with their start and end apart: 5, of which 5 were waited for; matrix products, arithmetic and copies ran while one was open for 42% of the time, Pallas kernels for 0%

profile of v1, /device:TPU:107, one launch (start us, length us, event | category | flops | bytes accessed | tf_op | source)
XLA Modules:
  0.0 1112.0 jit_solution(14630787674965145102)
XLA Ops:
  32.6 12.4 %copy.62 = bf16[2048,16,128]{0,2,1:T(8,128)(2,1)} copy(bf16[2048,16,128]{2,1,0:T(8,128)(2,1)} %param.21) | data formatting | bytes 16777216 | tf_op args[7]
  87.5 53.7 %all-reduce.3.cloned.1.call-done = (bf16[2048,1024]{1,0:T(8,128)(2,1)}, bf16[2048,1024]{1,0:T(8,128)(2,1)}, bf16[1024,2048]{1,0:T(8,128)(2,1)}) async-done(((bf16[2048,1024]{1,0:T(8,128)(2,1)}, bf16[2048,1024]{1,0:T(8,128)(2,1)}, bf16[1024,2048]{1,0:T(8,128)(2,1)}), (bf16[2048,1024]{1,0:T(8,128)(2,1)}, bf16[2048,1024]{1,0:T(8,128)(2,1)}, bf16[1024,2048]{1,0:T(8,128)(2,1)})) %all-reduce.3.cloned.1.call-update) | async-done | bytes 12582928 | tf_op jit(solution)/shard_map/psum | solution.py:94
  171.8 23.9 %fusion.165 = (f32[16,384]{1,0:T(8,128)S(1)}, f32[16,384,768]{2,1,0:T(8,128)}) fusion(f32[16,384,768]{2,1,0:T(8,128)} %fusion.63, pred[384,768]{1,0:T(8,128)(4,1)S(1)} %copy-done.10), kind=kOutput, calls=%fused_computation.218 | output fusion | flops 28312320 | bytes 38068224 | tf_op jit(solution)/shard_map/sub | solution.py:49
  195.6 13.6 %fusion.49 = (f32[384]{0:T(512)S(1)}, bf16[384,2048]{1,0:T(8,128)(2,1)S(1)}) fusion(bf16[16,128,2048]{2,1,0:T(8,128)(2,1)} %param.23, f32[16,384,768]{2,1,0:T(8,128)} %get-tuple-element.69, f32[16,384]{1,0:T(8,128)S(1)} %get-tuple-element.68, bf16[384,16,128]{2,0,1:T(8,128)(2,1)} %fusion.89, bf16[384,16,128]{2,0,1:T(8,128)(2,1)} %fusion.86, ...), kind=kOutput, calls=%fused_computation.81 | convolution fusion | flops 4450418176 | bytes 33580544 | tf_op jit(solution)/shard_map/qhk,hkd->qd/dot_general | solution.py:51
  211.5 14.8 %all_to_all.33 = s32[32,2,768]{2,1,0:T(2,128)S(1)} all-to-all(s32[32,2,768]{2,1,0:T(2,128)S(1)} %all_to_all.22), channel_id=1, replica_groups=mesh['data'=1,'expert'=32] {'expert'}, dimensions={0} | all-to-all | bytes 393216 | tf_op jit(solution)/shard_map/all_to_all | solution.py:102
  227.1 69.4 %all-gather.5.cloned.1.call-done = bf16[12288,2048]{1,0:T(8,128)(2,1)} async-done(((bf16[384,2048]{1,0:T(8,128)(2,1)}), bf16[12288,2048]{1,0:T(8,128)(2,1)}) %all-gather.5.cloned.1.call-update) | async-done | bytes 50331664 | tf_op jit(solution)/shard_map/all_gather | solution.py:115
  296.6 23.1 %fusion.18 = bf16[32,136,2048]{2,1,0:T(8,128)(2,1)} fusion(bf16[32,384,2048]{2,1,0:T(8,128)(2,1)} %bitcast.177, s32[32,384]{1,0:T(8,128)S(1)} %get-tuple-element.83), kind=kOutput, calls=%fused_computation.38 | convolution fusion | flops 6846775296 | bytes 68206592 | tf_op jit(solution)/shard_map/srt,std->srd/dot_general | solution.py:118
  319.7 130.2 %all-gather.7.cloned.1.call-done = bf16[12288,2048]{1,0:T(8,128)(2,1)} async-done(((bf16[384,2048]{1,0:T(8,128)(2,1)}), bf16[12288,2048]{1,0:T(8,128)(2,1)}) %all-gather.7.cloned.1.call-update) | async-done | bytes 50331664 | tf_op jit(solution)/shard_map/all_gather | solution.py:115
  449.9 30.0 %convert_add_fusion.1 = bf16[32,136,2048]{2,1,0:T(8,128)(2,1)} fusion(bf16[32,136,2048]{2,1,0:T(8,128)(2,1)} %fusion.18, bf16[32,384,2048]{2,1,0:T(8,128)(2,1)} %bitcast.179, s32[32,384]{1,0:T(8,128)S(1)} %get-tuple-element.82), kind=kOutput, calls=%fused_computation.12 | convolution fusion | flops 6864601088 | bytes 86032384 | tf_op jit(solution)/shard_map/srt,std->srd/dot_general | solution.py:118
  479.9 24.9 %fusion.27 = f32[4352,1024]{1,0:T(8,128)} fusion(bf16[4352,2048]{1,0:T(8,128)(2,1)} %bitcast.188, bf16[2,2048,1024]{2,1,0:T(8,128)(2,1)} %param.25), kind=kOutput, calls=%fused_computation.55 | convolution fusion | flops 18253611008 | bytes 39845888 | tf_op jit(solution)/shard_map/dot_general | solution.py:61
  504.8 28.8 %multiply_convert_fusion.1.clone.5 = bf16[4352,1024]{1,0:T(8,128)(2,1)} fusion(f32[4352,1024]{1,0:T(8,128)} %fusion.27, bf16[4352,2048]{1,0:T(8,128)(2,1)} %bitcast.189, bf16[2,2048,1024]{2,1,0:T(8,128)(2,1)} %param.26), kind=kOutput, calls=%fused_computation.11.clone.clone.clone.2 | convolution fusion | flops 18280349696 | bytes 48758784 | tf_op jit(solution)/shard_map/dot_general | solution.py:62
  533.6 25.0 %convolution_convert_fusion.1 = bf16[4352,2048]{1,0:T(8,128)(2,1)} fusion(bf16[2,1024,2048]{2,1,0:T(8,128)(2,1)S(1)} %bitcast.203, bf16[4352,1024]{1,0:T(8,128)(2,1)} %multiply_convert_fusion.1.clone.5), kind=kOutput, calls=%fused_computation.5 | convolution fusion | flops 18262523904 | bytes 30932992 | tf_op jit(solution)/shard_map/dot_general | solution.py:64
  565.6 23.1 %fusion.19 = bf16[32,136,2048]{2,1,0:T(8,128)(2,1)} fusion(bf16[32,384,2048]{2,1,0:T(8,128)(2,1)} %bitcast.178, s32[32,384]{1,0:T(8,128)S(1)} %copy-done.12), kind=kOutput, calls=%fused_computation.39 | convolution fusion | flops 6846775296 | bytes 68206592 | tf_op jit(solution)/shard_map/srt,std->srd/dot_general | solution.py:118
  588.7 30.0 %convert_add_fusion = bf16[32,136,2048]{2,1,0:T(8,128)(2,1)} fusion(bf16[32,136,2048]{2,1,0:T(8,128)(2,1)} %fusion.19, bf16[32,384,2048]{2,1,0:T(8,128)(2,1)} %bitcast.180, s32[32,384]{1,0:T(8,128)S(1)} %copy-done.11), kind=kOutput, calls=%fused_computation.10 | convolution fusion | flops 6864601088 | bytes 86032384 | tf_op jit(solution)/shard_map/srt,std->srd/dot_general | solution.py:118
  618.7 24.9 %fusion.32 = f32[4352,1024]{1,0:T(8,128)} fusion(bf16[4352,2048]{1,0:T(8,128)(2,1)} %bitcast.186, bf16[2,2048,1024]{2,1,0:T(8,128)(2,1)} %param.25), kind=kOutput, calls=%fused_computation.61 | convolution fusion | flops 18253611008 | bytes 39845888 | tf_op jit(solution)/shard_map/dot_general | solution.py:61
  643.6 29.0 %multiply_convert_fusion.clone.5 = bf16[4352,1024]{1,0:T(8,128)(2,1)} fusion(f32[4352,1024]{1,0:T(8,128)} %fusion.32, bf16[4352,2048]{1,0:T(8,128)(2,1)} %bitcast.187, bf16[2,2048,1024]{2,1,0:T(8,128)(2,1)} %param.26), kind=kOutput, calls=%fused_computation.9.clone.clone.clone.2 | convolution fusion | flops 18280349696 | bytes 48758784 | tf_op jit(solution)/shard_map/dot_general | solution.py:62
  672.6 25.1 %convolution_convert_fusion = bf16[4352,2048]{1,0:T(8,128)(2,1)} fusion(bf16[2,1024,2048]{2,1,0:T(8,128)(2,1)S(1)} %bitcast.205, bf16[4352,1024]{1,0:T(8,128)(2,1)} %multiply_convert_fusion.clone.5), kind=kOutput, calls=%fused_computation.4 | convolution fusion | flops 18262523904 | bytes 30932992 | tf_op jit(solution)/shard_map/dot_general | solution.py:64
  697.8 104.8 %all-to-all-done.1 = bf16[32,136,2048]{2,1,0:T(8,128)(2,1)} async-done(((bf16[32,136,2048]{2,1,0:T(8,128)(2,1)}), bf16[32,136,2048]{2,1,0:T(8,128)(2,1)}, u32[]{:S(2)}, u32[]{:S(2)}) %all-to-all-start.1) | async-done | bytes 17825824 | tf_op jit(solution)/shard_map/all_to_all | solution.py:131
  827.3 24.9 %copy.75 = bf16[2304,4352]{1,0:T(8,128)(2,1)} copy(bf16[2304,4352]{0,1:T(8,128)(2,1)} %pad_maximum_fusion) | data formatting | bytes 40108032 | tf_op jit(solution)/shard_map/concatenate | solution.py:75
  852.3 16.5 %pad_maximum_fusion.1 = bf16[2304,4352]{0,1:T(8,128)(2,1)} fusion(bf16[768,4352]{0,1:T(8,128)(2,1)} %get-tuple-element.52, bf16[768,4352]{0,1:T(8,128)(2,1)} %get-tuple-element.51, bf16[768,4352]{0,1:T(8,128)(2,1)} %get-tuple-element.53), kind=kLoop, calls=%fused_computation.3 | loop fusion | flops 60162048 | bytes 40108032 | tf_op jit(solution)/shard_map/concatenate | solution.py:75
  868.8 25.1 %copy.76 = bf16[2304,4352]{1,0:T(8,128)(2,1)} copy(bf16[2304,4352]{0,1:T(8,128)(2,1)} %pad_maximum_fusion.1) | data formatting | bytes 40108032 | tf_op jit(solution)/shard_map/concatenate | solution.py:75
  926.0 51.4 %convolution_reduce_fusion.1 = f32[768,2048]{1,0:T(8,128)} fusion(bf16[3,768,4352]{2,1,0:T(8,128)(2,1)} %bitcast.182, bf16[4352,2048,1]{1,0,2:T(8,128)(2,1)} %bitcast.32), kind=kOutput, calls=%fused_computation.52 | convolution fusion | flops 41073770496 | bytes 44171264 | tf_op jit(solution)/shard_map/dot_general | solution.py:76
  977.4 66.1 %all-to-all-done.2 = bf16[32,136,2048]{2,1,0:T(8,128)(2,1)} async-done(((bf16[32,136,2048]{2,1,0:T(8,128)(2,1)}), bf16[32,136,2048]{2,1,0:T(8,128)(2,1)}, u32[]{:S(2)}, u32[]{:S(2)}) %all-to-all-start.2) | async-done | bytes 17825824 | tf_op jit(solution)/shard_map/all_to_all | solution.py:131
  1043.5 51.7 %convolution_reduce_fusion = f32[768,2048]{1,0:T(8,128)} fusion(bf16[3,768,4352]{2,1,0:T(8,128)(2,1)} %bitcast.181, bf16[4352,2048,1]{1,0,2:T(8,128)(2,1)} %bitcast.41), kind=kOutput, calls=%fused_computation.51 | convolution fusion | flops 41073770496 | bytes 44171264 | tf_op jit(solution)/shard_map/dot_general | solution.py:76
  (138 shorter events, 175.3 us)
Async XLA Ops:
  6.5 134.6 %all-reduce.3.cloned.1.call-start = ((), (), s32[]{:S(2)}) async-start(), calls=%async_computation.5 | async-start | bytes 25165824 | tf_op jit(solution)/shard_map/psum | solution.py:94
  18.0 278.5 %all-gather.5.cloned.1.call-start = ((), (), s32[]{:S(2)}) async-start(), calls=%async_computation.3 | async-start | bytes 51904512 | tf_op jit(solution)/shard_map/all_gather | solution.py:115
  32.6 13.2 %copy-start.21 = (f32[2048]{0:T(1024)S(1)}, f32[2048]{0:T(1024)}, u32[]{:S(2)}) copy-start(f32[2048]{0:T(1024)} %param.19) | copy-start | bytes 24580
  45.0 8.3 slice-start
  45.8 7.5 slice-start.1
  74.0 11.9 %copy-start.15 = (f32[2048]{0:T(1024)S(1)}, f32[2048]{0:T(1024)}, u32[]{:S(2)}) copy-start(f32[2048]{0:T(1024)} %param.24) | copy-start | bytes 24580
  141.2 308.7 %all-gather.7.cloned.1.call-start = ((), (), s32[]{:S(2)}) async-start(), calls=%async_computation.4 | async-start | bytes 51904512 | tf_op jit(solution)/shard_map/all_gather | solution.py:115
  141.3 10.4 slice-start.2
  144.3 7.4 slice-start.3
  156.4 8.9 slice-start.8
  157.5 7.9 slice-start.9
  211.4 108.3 %copy-start.5 = (s32[768,64]{0,1:T(8,128)}, s32[768,64]{0,1:T(8,128)S(1)}, u32[]{:S(2)}) copy-start(s32[768,64]{0,1:T(8,128)S(1)} %fusion.125) | copy-start | bytes 589828
  479.9 53.7 %slice-start.4 = ((s8[8388608]{0:T(1024)(128)(4,1)}), s8[4194304]{0:T(1024)(128)(4,1)S(1)}, s32[]{:S(2)}) async-start(s8[8388608]{0:T(1024)(128)(4,1)} %bitcast.202), calls=%async_computation.10 | async-start | bytes 8388608
  504.8 28.8 %slice-start.5 = ((s8[8388608]{0:T(1024)(128)(4,1)}), s8[4194304]{0:T(1024)(128)(4,1)S(1)}, s32[]{:S(2)}) async-start(s8[8388608]{0:T(1024)(128)(4,1)} %bitcast.202), calls=%async_computation.11 | async-start | bytes 8388608
  558.6 6.9 copy-start.12
  558.6 243.9 %all-to-all-start.1 = ((bf16[32,136,2048]{2,1,0:T(8,128)(2,1)}), bf16[32,136,2048]{2,1,0:T(8,128)(2,1)}, u32[]{:S(2)}, u32[]{:S(2)}) async-start(bf16[32,136,2048]{2,1,0:T(8,128)(2,1)} %bitcast.185), calls=%async_computation.1 | async-start | bytes 35651584 | tf_op jit(solution)/shard_map/all_to_all | solution.py:131
  565.6 23.1 %copy-start.11 = (s32[32,384]{1,0:T(8,128)S(1)}, s32[32,384]{1,0:T(8,128)}, u32[]{:S(2)}) copy-start(s32[32,384]{1,0:T(8,128)} %get-tuple-element.80) | copy-start | bytes 147460
  618.7 53.9 %slice-start.6 = ((s8[8388608]{0:T(1024)(128)(4,1)}), s8[4194304]{0:T(1024)(128)(4,1)S(1)}, s32[]{:S(2)}) async-start(s8[8388608]{0:T(1024)(128)(4,1)} %bitcast.204), calls=%async_computation.12 | async-start | bytes 8388608
  643.6 29.0 %slice-start.7 = ((s8[8388608]{0:T(1024)(128)(4,1)}), s8[4194304]{0:T(1024)(128)(4,1)S(1)}, s32[]{:S(2)}) async-start(s8[8388608]{0:T(1024)(128)(4,1)} %bitcast.204), calls=%async_computation.13 | async-start | bytes 8388608
  802.6 241.0 %all-to-all-start.2 = ((bf16[32,136,2048]{2,1,0:T(8,128)(2,1)}), bf16[32,136,2048]{2,1,0:T(8,128)(2,1)}, u32[]{:S(2)}, u32[]{:S(2)}) async-start(bf16[32,136,2048]{2,1,0:T(8,128)(2,1)} %bitcast.184), calls=%async_computation.2 | async-start | bytes 35651584 | tf_op jit(solution)/shard_map/all_to_all | solution.py:131
  868.8 25.1 %copy-start.18 = (f32[384]{0:T(512)S(1)}, f32[384]{0:T(512)}, u32[]{:S(2)}) copy-start(f32[384]{0:T(512)} %param.18) | copy-start | bytes 4612
  868.8 25.1 %copy-start.17 = (s32[384]{0:T(512)S(1)}, s32[384]{0:T(512)}, u32[]{:S(2)}) copy-start(s32[384]{0:T(512)} %param.17) | copy-start | bytes 4612
  868.8 26.7 %copy-start = (bf16[384,2048]{1,0:T(8,128)(2,1)S(1)}, bf16[384,2048]{1,0:T(8,128)(2,1)}, u32[]{:S(2)}) copy-start(bf16[384,2048]{1,0:T(8,128)(2,1)} %fusion.48) | copy-start | bytes 4718596
  868.8 26.7 %copy-start.1 = (bf16[384,2048]{1,0:T(8,128)(2,1)S(1)}, bf16[384,2048]{1,0:T(8,128)(2,1)}, u32[]{:S(2)}) copy-start(bf16[384,2048]{1,0:T(8,128)(2,1)} %fusion.51) | copy-start | bytes 4718596
  (13 other events, 45.8 us)
Sparse Core Ops, SparseCore 0:
  18.1 123.0 all-reduce.2
  143.3 153.2 all-gather.4
  298.6 151.2 all-gather.6

commit v2 on v1

--- a/solution.py
+++ b/solution.py
@@ -1,12 +1,17 @@
+import functools
+import math
+
 import jax
 import jax.numpy as jnp
 from jax import lax
+from jax.experimental import pallas as pl
+from jax.experimental.pallas import tpu as pltpu
 from jax.sharding import PartitionSpec as P
 
 EPS = 1e-6
 ROPE_BASE = 10000.0
 HOT_ID = 1
-CHUNKS = 2
+CHUNKS = 1
 F32 = jnp.float32
 BF16 = jnp.bfloat16
 
@@ -77,6 +82,222 @@
     return jnp.sum(out.reshape(len(g_parts), -1, out.shape[-1]), axis=0)
 
 
+def _up(v, m):
+    return (v + m - 1) // m * m
+
+
+def _exchange(n, axis, theirs, u_all, w1, w3, w2, gates, y0,
+              y_out, recv, stage,
+              ubuf, v1, v3, v2, xin, z, out, y, gbuf, rbuf,
+              u_sem, w_sem, o_sem, y_sem, g_sem, r_sem, send_sem, recv_sem):
+    T, D = y.shape
+    el, CP = 2, xin.shape[1] // 4
+    C2 = recv.shape[1]
+    C = C2 // 2
+    FF = z.shape[2]
+    side = math.isqrt(n // 2)
+    FT, NT = min(256, FF), min(256, D)
+    me = lax.axis_index(axis)
+    core, chip = lax.rem(me, 2), lax.div(me, 2)
+    cx, cy = lax.rem(chip, side), lax.div(chip, side)
+
+    def chip_at(o, sign):
+        dx = lax.rem(o + 1, side)
+        dy = lax.rem(o + 1 + lax.div(o, side), side)
+        px = lax.rem(cx + sign * dx + side, side)
+        py = lax.rem(cy + sign * dy + side, side)
+        return py * side + px
+
+    def dest(k):
+        return chip_at(lax.div(k, 2), 1) * 2 + lax.rem(k, 2)
+
+    def u_copy(k, slot):
+        return pltpu.make_async_copy(u_all.at[dest(k)], ubuf.at[slot], u_sem.at[slot])
+
+    def g_copy(c, slot):
+        return pltpu.make_async_copy(gates.at[chip_at(c, -1)], gbuf.at[slot], g_sem.at[slot])
+
+    def send(d):
+        return pltpu.make_async_remote_copy(
+            src_ref=stage.at[d], dst_ref=recv.at[me],
+            send_sem=send_sem.at[d], recv_sem=recv_sem.at[me],
+            device_id={axis: d}, device_id_type=pl.DeviceIdType.MESH)
+
+    weights = [pltpu.make_async_copy(a, b, w_sem.at[i])
+               for i, (a, b) in enumerate(((w1, v1), (w3, v3), (w2, v2)))]
+    u_copy(0, 0).start()
+    u_copy(1, 1).start()
+    for cp in weights:
+        cp.start()
+    y_copy = pltpu.make_async_copy(y0, y, y_sem.at[0])
+    y_copy.start()
+    g_copy(0, 0).start()
+
+    barrier = pltpu.get_barrier_semaphore()
+
+    @pl.loop(1, n)
+    def _(k):
+        pl.semaphore_signal(barrier, inc=1, device_id={axis: lax.rem(me + k, n)},
+                            device_id_type=pl.DeviceIdType.MESH)
+
+    pl.semaphore_wait(barrier, n - 1)
+    rbuf[:, 2 * C2:, :] = jnp.zeros((2, rbuf.shape[1] - 2 * C2, D), BF16)
+
+    @pl.loop(0, n // 4)
+    def _(b):
+        for j in range(4):
+            k = b * 4 + j
+            slot = j % 2
+            u_copy(k, slot).wait()
+            where = theirs[dest(k)]
+            rows = lax.broadcasted_iota(jnp.int32, (CP, T), 0)
+            pick = [(where[l:l + 1, :] == rows).astype(F32).astype(BF16) for l in range(el)]
+
+            @pl.loop(0, D // NT)
+            def _(i):
+                cols = pl.ds(pl.multiple_of(i * NT, NT), NT)
+                for l in range(el):
+                    xin[l, j * CP:(j + 1) * CP, cols] = jnp.dot(
+                        pick[l], ubuf[slot, :, cols], preferred_element_type=F32).astype(BF16)
+
+            @pl.when(k + 2 < n)
+            def _():
+                u_copy(k + 2, slot).start()
+
+        @pl.when(b == 0)
+        def _():
+            for cp in weights:
+                cp.wait()
+
+        for l in range(el):
+            @pl.loop(0, FF // FT)
+            def _(i):
+                cols = pl.ds(pl.multiple_of(i * FT, FT), FT)
+                h1 = jnp.dot(xin[l], v1[l, :, cols], preferred_element_type=F32)
+                h3 = jnp.dot(xin[l], v3[l, :, cols], preferred_element_type=F32)
+                z[l, :, cols] = (h1 * jax.nn.sigmoid(h1) * h3).astype(BF16)
+
+        @pl.loop(0, D // NT)
+        def _(i):
+            cols = pl.ds(pl.multiple_of(i * NT, NT), NT)
+            o0 = jnp.dot(z[0], v2[0, :, cols], preferred_element_type=F32)
+            o1 = jnp.dot(z[1], v2[1, :, cols], preferred_element_type=F32)
+            for j in range(4):
+                both = jnp.concatenate([o0[j * CP:j * CP + C], o1[j * CP:j * CP + C]], axis=0)
+                out[j, :, cols] = both.astype(BF16)
+
+        for j in range(4):
+            d = dest(b * 4 + j)
+
+            @pl.when(d != me)
+            def _():
+                pltpu.make_async_copy(out.at[j], stage.at[d], o_sem.at[j]).start()
+
+            @pl.when(d == me)
+            def _():
+                pltpu.make_async_copy(out.at[j], recv.at[me], o_sem.at[j]).start()
+
+        for j in range(4):
+            d = dest(b * 4 + j)
+
+            @pl.when(d != me)
+            def _():
+                pltpu.make_async_copy(out.at[j], stage.at[d], o_sem.at[j]).wait()
+                send(d).start()
+
+            @pl.when(d == me)
+            def _():
+                pltpu.make_async_copy(out.at[j], recv.at[me], o_sem.at[j]).wait()
+
+    y_copy.wait()
+
+    def from_chip(c, slot):
+        e = chip_at(c, -1) * 2
+        return e, [pltpu.make_async_copy(recv.at[e + i], rbuf.at[slot, i * C2:(i + 1) * C2], r_sem.at[slot, i])
+                   for i in range(2)]
+
+    @pl.loop(0, n // 4)
+    def _(cc):
+        for slot in range(2):
+            c = cc * 2 + slot
+            e, copies = from_chip(c, slot)
+            for i in range(2):
+                @pl.when(e + i != me)
+                def _():
+                    pltpu.make_async_remote_copy(
+                        src_ref=stage.at[e + i], dst_ref=recv.at[e + i],
+                        send_sem=send_sem.at[e + i], recv_sem=recv_sem.at[e + i],
+                        device_id={axis: me}, device_id_type=pl.DeviceIdType.MESH).wait_recv()
+                copies[i].start()
+
+            @pl.when(c + 1 < n // 2)
+            def _():
+                g_copy(c + 1, 1 - slot).start()
+
+            g_copy(c, slot).wait()
+            for cp in copies:
+                cp.wait()
+
+            @pl.loop(0, D // NT)
+            def _(i):
+                cols = pl.ds(pl.multiple_of(i * NT, NT), NT)
+                acc = y[:, cols]
+                for p in range(3):
+                    acc = acc + jnp.dot(gbuf[slot, p], rbuf[slot, :, cols], preferred_element_type=F32)
+                y[:, cols] = acc
+
+    @pl.loop(0, D // NT)
+    def _(i):
+        cols = pl.ds(pl.multiple_of(i * NT, NT), NT)
+        ubuf[0, :, cols] = y[:, cols].astype(BF16)
+
+    done = pltpu.make_async_copy(ubuf.at[0], y_out, y_sem.at[0])
+    done.start()
+    done.wait()
+
+    @pl.loop(0, n)
+    def _(d):
+        @pl.when(d != me)
+        def _():
+            send(d).wait_send()
+
+
+def _run_exchange(n, axis, C, theirs, u_all, w1, w3, w2, gates, y0):
+    T, D = y0.shape
+    el, _, FF = w1.shape
+    C2, CP = 2 * C, _up(C, 16)
+    KP = gates.shape[-1]
+    any_spec = pl.BlockSpec(memory_space=pl.ANY)
+    dma = pltpu.SemaphoreType.DMA
+    rows = n * 2 * C
+    return pl.pallas_call(
+        functools.partial(_exchange, n, axis),
+        out_shape=(jax.ShapeDtypeStruct((T, D), BF16),
+                   jax.ShapeDtypeStruct((n, C2, D), BF16),
+                   jax.ShapeDtypeStruct((n, C2, D), BF16)),
+        in_specs=[pl.BlockSpec(memory_space=pltpu.VMEM)] + [any_spec] * 6,
+        out_specs=(any_spec,) * 3,
+        scratch_shapes=[
+            pltpu.VMEM((2, T, D), BF16),
+            pltpu.VMEM((el, D, FF), BF16),
+            pltpu.VMEM((el, D, FF), BF16),
+            pltpu.VMEM((el, FF, D), BF16),
+            pltpu.VMEM((el, 4 * CP, D), BF16),
+            pltpu.VMEM((el, 4 * CP, FF), BF16),
+            pltpu.VMEM((4, C2, D), BF16),
+            pltpu.VMEM((T, D), F32),
+            pltpu.VMEM((2, 3, T, KP), BF16),
+            pltpu.VMEM((2, KP, D), BF16),
+            dma((2,)), dma((3,)), dma((4,)), dma((1,)), dma((2,)), dma((2, 2)), dma((n,)), dma((n,)),
+        ],
+        compiler_params=pltpu.CompilerParams(
+            collective_id=0, has_side_effects=True, vmem_limit_bytes=66 * 1000 * 1000),
+        cost_estimate=pl.CostEstimate(
+            flops=rows * 6 * D * FF + rows * 8 * T * D, bytes_accessed=rows * D * 8, transcendentals=rows * FF),
+        name='exchange',
+    )(theirs, u_all, w1, w3, w2, gates, y0)[0]
+
+
 def solution(mesh):
     n = mesh.shape['expert']
 
@@ -100,40 +321,28 @@
         upto = jnp.dot(tri, has.astype(BF16), preferred_element_type=F32)
         place = jnp.where(has, upto.astype(jnp.int32) - 1, -1)
         theirs = lax.all_to_all(place.T, 'expert', 0, 0, tiled=True).reshape(n, el, T)
-
-        step = T // CHUNKS
-        us = []
-        xin = [None] * el
-        slot = jnp.arange(C, dtype=jnp.int32)
+        theirs = jnp.pad(theirs, ((0, 0), (0, 8 - el), (0, 0)), constant_values=-1)
+
+        per = 2 * el
+        col = jnp.arange(_up(per * C, 128), dtype=jnp.int32)
+        key = jnp.where(has, place + (jnp.arange(E, dtype=jnp.int32) % per) * C, -1)
+        key = key.reshape(T, E // per, per).transpose(1, 0, 2)
+        parts = jnp.stack(_parts(gate)).reshape(3, T, E // per, per).transpose(2, 0, 1, 3)
+        gates = jnp.zeros((), BF16)
+        for k in range(per):
+            hit = key[:, None, :, k, None] == col
+            gates = jnp.where(hit, parts[:, :, :, k, None], gates)
+
         chunks = _attention_chunks(x, ln1, wq, wk, wv, wo, CHUNKS)
-        u = None
-        for c in range(CHUNKS):
-            u = _rms(chunks.send(u), ln2)
-            if c == 0:
-                u, *hw = lax.optimization_barrier((u, *hw))
-            us.append(u)
-            every = lax.all_gather(u, 'expert')
-            for l in range(el):
-                pick = (theirs[:, l, None, c * step:(c + 1) * step] == slot[:, None]).astype(BF16)
-                part = jnp.einsum('srt,std->srd', pick, every, preferred_element_type=F32).astype(BF16)
-                xin[l] = part if xin[l] is None else xin[l] + part
-        u = jnp.concatenate(us, axis=0)
-
-        y = jnp.zeros((T, D), F32)
+        u = _rms(chunks.send(None), ln2)
+        u, *hw = lax.optimization_barrier((u, *hw))
+        u_all = lax.all_gather(u, 'expert')
+
         hot_hit = hot_tok[:, None] == jnp.arange(T, dtype=jnp.int32)
         hot_rows = jnp.dot(hot_hit.astype(BF16), u, preferred_element_type=F32).astype(BF16)
         hot_out = _ffn(hot_rows, *hw)
-        y = y + _gated([v[None, :] for v in _parts(hot_g)], hot_hit.T, hot_out)
-
-        g_parts = _parts(gate)
-        for l in range(el):
-            out = _ffn(xin[l].reshape(n * C, D), w1[l], w3[l], w2[l])
-            back = lax.all_to_all(out, 'expert', 0, 0, tiled=True)
-            hit = (place.reshape(T, n, el)[:, :, l, None] == slot).reshape(T, n * C)
-            gl = [jnp.broadcast_to(v.reshape(T, n, el)[:, :, l, None], (T, n, C)).reshape(T, n * C)
-                  for v in g_parts]
-            y = y + _gated(gl, hit, back)
-        return y.astype(BF16)
+        y0 = _gated([v[None, :] for v in _parts(hot_g)], hot_hit.T, hot_out)
+        return _run_exchange(n, 'expert', C, theirs, u_all, w1, w3, w2, gates, y0)
 
     tk = ('data', 'expert')
     rep3 = P(None, None, None)

time: 1120 us -> 1160 us (1.036)
  the two profiles are of different devices: /device:TPU:107 before, /device:TPU:97 now
where the time goes in v2:
time: 1160 us; the launch traced here: 1150 us
  Pallas kernels  706 us (61%)
  waiting for transfers between devices  196 us (17%)
  other arithmetic  99 us (9%)
  matrix products  90.8 us (8%)
  local copies, waits for them, and re-layouts  34.9 us (3%)
  between operations  14.1 us (1%)
    pallas_call x1, Pallas kernels, _run_exchange(): pl.pallas_call(functools.partial(_exchange, n, axis), out_shape=(jax.Shap...  706 us
    all_gather x1, waiting for transfers between devices, local(): u_all = lax.all_gather(u, 'expert')  176 us
    select_n x1, other arithmetic, local(): gates = jnp.where(hit, parts[:, :, :, k, None], gates)  41.2 us
    unnamed x29, local copies, waits for them, and re-layouts  31.4 us
    eq x4, other arithmetic, local(): hit = key[:, None, :, k, None] == col  24.2 us
  transfers between devices with their start and end apart: 3, of which 2 were waited for; matrix products, arithmetic and copies ran while one was open for 18% of the time, Pallas kernels for 0%

profile of v2, /device:TPU:97, one launch (start us, length us, event | category | flops | bytes accessed | tf_op | source)
XLA Modules:
  0.0 1146.2 jit_solution(17786209207885458102)
XLA Ops:
  6.6 4.7 select_bitcast_fusion
  12.7 5.1 select_bitcast_fusion.1
  21.4 12.4 %copy.46 = bf16[2048,16,128]{0,2,1:T(8,128)(2,1)} copy(bf16[2048,16,128]{2,1,0:T(8,128)(2,1)} %param.20) | data formatting | bytes 16777216 | tf_op args[6]
  33.8 10.4 fusion.8
  44.2 9.0 fusion.63
  53.2 12.4 %copy.47 = bf16[2048,16,128]{0,2,1:T(8,128)(2,1)} copy(bf16[2048,16,128]{2,1,0:T(8,128)(2,1)} %param.21) | data formatting | bytes 16777216 | tf_op args[7]
  65.5 9.4 fusion.61
  75.0 3.9 subtract_convert_fusion.1
  78.9 19.0 %fusion.68 = (f32[16,768]{1,0:T(8,128)S(1)}, f32[16,768,768]{1,2,0:T(8,128)}) fusion(pred[768,768]{0,1:T(8,128)(4,1)} %iota_compare_fusion.4, bf16[768,16,64]{0,2,1:T(8,128)(2,1)} %get-tuple-element.22, bf16[768,16,64]{0,2,1:T(8,128)(2,1)} %get-tuple-element.23, bf16[768,16,64]{0,2,1:T(8,128)(2,1)} %get-tuple-element.19, ...), kind=kOutput, calls=%fused_computation.108 | convolution fusion | flops 2466251520 | bytes 44679168 | tf_op jit(solution)/shard_map/sub | solution.py:54
  97.9 21.5 %fusion.10 = (f32[768]{0:T(1024)S(1)}, bf16[768,2048]{1,0:T(8,128)(2,1)}) fusion(bf16[16,128,2048]{2,1,0:T(8,128)(2,1)} %param.23, f32[16,768,768]{1,2,0:T(8,128)} %get-tuple-element.44, f32[16,768]{1,0:T(8,128)S(1)} %get-tuple-element.43, bf16[768,16,128]{2,0,1:T(8,128)(2,1)} %fusion.8, bf16[768,2048]{1,0:T(8,128)(2,1)S(1)} %copy-done.2), kind=kOutput, calls=%fused_computation.22 | convolution fusion | flops 8888253440 | bytes 55626752 | tf_op jit(solution)/shard_map/qhk,hkd->qd/dot_general | solution.py:56
  119.4 4.3 fusion.12
  123.8 19.8 %all-reduce.4.cloned.1.call-done = (bf16[2048,1024]{1,0:T(8,128)(2,1)}, bf16[2048,1024]{1,0:T(8,128)(2,1)}, bf16[1024,2048]{1,0:T(8,128)(2,1)}) async-done(((bf16[2048,1024]{1,0:T(8,128)(2,1)}, bf16[2048,1024]{1,0:T(8,128)(2,1)}, bf16[1024,2048]{1,0:T(8,128)(2,1)}), (bf16[2048,1024]{1,0:T(8,128)(2,1)}, bf16[2048,1024]{1,0:T(8,128)(2,1)}, bf16[1024,2048]{1,0:T(8,128)(2,1)})) %all-reduce.4.cloned.1.call-update) | async-done | bytes 12582928 | tf_op jit(solution)/shard_map/psum | solution.py:315
  144.9 5.3 all-to-all-start
  152.6 5.0 iota_compare_fusion
  157.7 5.0 iota_compare_fusion.2
  162.7 7.0 iota_compare_fusion.1
  169.8 7.1 iota_compare_fusion.3
  176.8 41.2 %select_select_fusion.gates = bf16[16,3,768,640]{3,2,1,0:T(8,128)(2,1)} fusion(pred[16,768,640]{2,1,0:T(8,128)(4,1)S(1)} %iota_compare_fusion, pred[16,768,640]{2,1,0:T(8,128)(4,1)} %iota_compare_fusion.1, pred[16,768,640]{2,1,0:T(8,128)(4,1)S(1)} %iota_compare_fusion.2, pred[16,768,640]{2,1,0:T(8,128)(4,1)} %iota_compare_fusion.3, ...), kind=kLoop, calls=%fused_computation.1 | loop fusion | flops 94371840 | bytes 78938112 | tf_op jit(solution)/shard_map/jit(_where)/select_n | solution.py:334
  219.4 3.9 convolution_convert_fusion
  228.4 12.5 %fusion.22 = f32[2304,2048]{1,0:T(8,128)} fusion(bf16[384,1024]{1,0:T(8,128)(2,1)} %multiply_convert_fusion, bf16[1024,2048]{1,0:T(8,128)(2,1)} %get-tuple-element.13, bf16[768,384]{1,0:T(8,128)(2,1)S(1)} %get-tuple-element.36, bf16[768,384]{1,0:T(8,128)(2,1)S(1)} %get-tuple-element.37, bf16[768,384]{1,0:T(8,128)(2,1)S(1)} %get-tuple-element.35), kind=kOutput, calls=%fused_computation.44 | convolution fusion | flops 5240586240 | bytes 25624576 | tf_op jit(solution)/shard_map/dot_general | solution.py:81
  241.0 11.9 %reduce_sum.52.y0 = f32[768,2048]{1,0:T(8,128)} reduce(f32[3,768,2048]{2,1,0:T(8,128)} %bitcast.58, f32[]{:T(128)} %constant.21.clone.1), dimensions={0}, to_apply=%region_9.10 | reduce | flops 3145728 | bytes 25165828 | tf_op jit(solution)/shard_map/reduce_sum | solution.py:82
  252.9 175.8 %all-gather.3.cloned.1.call-done = bf16[24576,2048]{1,0:T(8,128)(2,1)} async-done(((bf16[768,2048]{1,0:T(8,128)(2,1)}), bf16[24576,2048]{1,0:T(8,128)(2,1)}) %all-gather.3.cloned.1.call-update) | async-done | bytes 100663312 | tf_op jit(solution)/shard_map/all_gather | solution.py:339
  428.7 706.2 %exchange.1 = (bf16[768,2048]{1,0:T(8,128)(2,1)}, bf16[32,272,2048]{2,1,0:T(8,128)(2,1)}, bf16[32,272,2048]{2,1,0:T(8,128)(2,1)}) custom-call(s32[32,8,768]{2,1,0:T(8,128)} %pad.4.theirs, bf16[32,768,2048]{2,1,0:T(8,128)(2,1)} %bitcast.11.u_all, bf16[2,2048,1024]{2,1,0:T(8,128)(2,1)} %w1.1, bf16[2,2048,1024]{2,1,0:T(8,128)(2,1)} %w3.1, ...), custom_call_target="tpu_custom_call" | custom-call | flops 219043332096 | bytes 142606336 | tf_op jit(solution)/shard_map/exchange/pallas_call | solution.py:273
  1134.9 4.0 copy.84
  (55 shorter events, 15.0 us)
Async XLA Ops:
  6.5 137.0 %all-reduce.4.cloned.1.call-start = ((), (), s32[]{:S(2)}) async-start(), calls=%async_computation.2 | async-start | bytes 25165824 | tf_op jit(solution)/shard_map/psum | solution.py:315
  6.6 6.2 copy-start.3
  17.8 2.1 copy-start.2
  17.9 410.8 %all-gather.3.cloned.1.call-start = ((), (), s32[]{:S(2)}) async-start(), calls=%async_computation.1 | async-start | bytes 103809024 | tf_op jit(solution)/shard_map/all_gather | solution.py:339
  21.4 12.4 %copy-start.11 = (f32[2048]{0:T(1024)S(1)}, f32[2048]{0:T(1024)}, u32[]{:S(2)}) copy-start(f32[2048]{0:T(1024)} %param.19) | copy-start | bytes 24580
  33.8 10.4 copy-start
  65.5 9.4 copy-start.1
  97.9 21.6 %copy-start.6 = (f32[2048]{0:T(1024)S(1)}, f32[2048]{0:T(1024)}, u32[]{:S(2)}) copy-start(f32[2048]{0:T(1024)} %param.24) | copy-start | bytes 24580
  119.4 24.2 %copy-start.4 = (s32[768,7]{0,1:T(8,128)S(1)}, s32[768,7]{0,1:T(8,128)}, u32[]{:S(2)}) copy-start(s32[768,7]{0,1:T(8,128)} %param.15) | copy-start | bytes 64516
  123.8 26.4 %copy-start.5 = (f32[768,7]{0,1:T(8,128)S(1)}, f32[768,7]{0,1:T(8,128)}, u32[]{:S(2)}) copy-start(f32[768,7]{0,1:T(8,128)} %param.16) | copy-start | bytes 64516
  143.5 7.3 copy-start.8
  144.9 73.6 %all-to-all-start = ((s32[32,2,768]{2,1,0:T(2,128)}), s32[32,2,768]{2,1,0:T(2,128)S(1)}, u32[]{:S(2)}, u32[]{:S(2)}) async-start(s32[32,2,768]{2,1,0:T(2,128)} %all_to_all.6), calls=%async_computation | async-start | bytes 393216 | tf_op jit(solution)/shard_map/all_to_all | solution.py:323
  176.8 41.2 %copy-start.7 = (s32[384]{0:T(512)S(1)}, s32[384]{0:T(512)}, u32[]{:S(2)}) copy-start(s32[384]{0:T(512)} %param.17) | copy-start | bytes 4612
  218.5 4.9 copy-start.10
  223.3 2.2 copy-start.9
Sparse Core Ops, SparseCore 0:
  18.0 125.4 all-reduce.3
  145.6 283.0 all-gather.2

commit v3 on v2

--- a/solution.py
+++ b/solution.py
@@ -86,36 +86,59 @@
     return (v + m - 1) // m * m
 
 
-def _exchange(n, axis, theirs, u_all, w1, w3, w2, gates, y0,
+ORDER4 = ((0, 1), (2, 0), (1, 3), (0, 2), (0, 0), (3, 0), (1, 1), (2, 1),
+          (0, 3), (3, 3), (3, 1), (1, 0), (2, 3), (3, 2), (2, 2), (1, 2))
+
+
+def _side(n):
+    return math.isqrt(n // 2)
+
+
+def _offset(side, o):
+    order = ORDER4 if side == 4 else tuple((i % side, i // side) for i in range(side * side))
+
+    def digit(vals):
+        lo, hi = (sum(v * 4 ** i for i, v in enumerate(vals[h * 8:h * 8 + 8])) for h in range(2))
+        q = lax.rem(o, 8)
+        power = ((1 + 3 * lax.rem(q, 2)) * (1 + 15 * lax.rem(lax.div(q, 2), 2)) * (1 + 255 * lax.div(q, 4)))
+        return lax.rem(lax.div(lo + lax.div(o, 8) * (hi - lo), power), 4)
+
+    return digit([v[0] for v in order]), digit([v[1] for v in order])
+
+
+def _peer(n, me, k, sending):
+    side = _side(n)
+    core, chip = lax.rem(me, 2), lax.div(me, 2)
+    other = lax.rem(k, 2)
+    dx, dy = _offset(side, lax.div(k, 2))
+    their = lax.rem(core + other, 2)
+    sign = 1 - 2 * core if sending else 2 * their - 1
+    px = lax.rem(lax.rem(chip, side) + sign * dx + side, side)
+    py = lax.rem(lax.div(chip, side) + sign * dy + side, side)
+    return (py * side + px) * 2 + their
+
+
+def _exchange(n, axis, theirs, u_all, w1, w3, w2, marks, y0,
               y_out, recv, stage,
-              ubuf, v1, v3, v2, xin, z, out, y, gbuf, rbuf,
-              u_sem, w_sem, o_sem, y_sem, g_sem, r_sem, send_sem, recv_sem):
+              ubuf, v1, v3, v2, xin, z, out, y, mbuf, sel, rbuf,
+              u_sem, w_sem, o_sem, y_sem, m_sem, r_sem, send_sem, recv_sem):
     T, D = y.shape
     el, CP = 2, xin.shape[1] // 4
     C2 = recv.shape[1]
     C = C2 // 2
     FF = z.shape[2]
-    side = math.isqrt(n // 2)
+    KW = sel.shape[2]
     FT, NT = min(256, FF), min(256, D)
     me = lax.axis_index(axis)
-    core, chip = lax.rem(me, 2), lax.div(me, 2)
-    cx, cy = lax.rem(chip, side), lax.div(chip, side)
-
-    def chip_at(o, sign):
-        dx = lax.rem(o + 1, side)
-        dy = lax.rem(o + 1 + lax.div(o, side), side)
-        px = lax.rem(cx + sign * dx + side, side)
-        py = lax.rem(cy + sign * dy + side, side)
-        return py * side + px
 
     def dest(k):
-        return chip_at(lax.div(k, 2), 1) * 2 + lax.rem(k, 2)
+        return _peer(n, me, k, True)
 
     def u_copy(k, slot):
         return pltpu.make_async_copy(u_all.at[dest(k)], ubuf.at[slot], u_sem.at[slot])
 
-    def g_copy(c, slot):
-        return pltpu.make_async_copy(gates.at[chip_at(c, -1)], gbuf.at[slot], g_sem.at[slot])
+    def m_copy(c, slot):
+        return pltpu.make_async_copy(marks.at[c], mbuf.at[slot], m_sem.at[slot])
 
     def send(d):
         return pltpu.make_async_remote_copy(
@@ -131,7 +154,7 @@
         cp.start()
     y_copy = pltpu.make_async_copy(y0, y, y_sem.at[0])
     y_copy.start()
-    g_copy(0, 0).start()
+    m_copy(0, 0).start()
 
     barrier = pltpu.get_barrier_semaphore()
 
@@ -141,7 +164,6 @@
                             device_id_type=pl.DeviceIdType.MESH)
 
     pl.semaphore_wait(barrier, n - 1)
-    rbuf[:, 2 * C2:, :] = jnp.zeros((2, rbuf.shape[1] - 2 * C2, D), BF16)
 
     @pl.loop(0, n // 4)
     def _(b):
@@ -211,30 +233,31 @@
 
     y_copy.wait()
 
-    def from_chip(c, slot):
-        e = chip_at(c, -1) * 2
-        return e, [pltpu.make_async_copy(recv.at[e + i], rbuf.at[slot, i * C2:(i + 1) * C2], r_sem.at[slot, i])
-                   for i in range(2)]
-
     @pl.loop(0, n // 4)
     def _(cc):
         for slot in range(2):
             c = cc * 2 + slot
-            e, copies = from_chip(c, slot)
+            copies = []
             for i in range(2):
-                @pl.when(e + i != me)
+                e = _peer(n, me, c * 2 + i, False)
+
+                @pl.when(e != me)
                 def _():
                     pltpu.make_async_remote_copy(
-                        src_ref=stage.at[e + i], dst_ref=recv.at[e + i],
-                        send_sem=send_sem.at[e + i], recv_sem=recv_sem.at[e + i],
+                        src_ref=stage.at[e], dst_ref=recv.at[e],
+                        send_sem=send_sem.at[e], recv_sem=recv_sem.at[e],
                         device_id={axis: me}, device_id_type=pl.DeviceIdType.MESH).wait_recv()
+                copies.append(pltpu.make_async_copy(recv.at[e], rbuf.at[slot, i], r_sem.at[slot, i]))
                 copies[i].start()
 
             @pl.when(c + 1 < n // 2)
             def _():
-                g_copy(c + 1, 1 - slot).start()
-
-            g_copy(c, slot).wait()
+                m_copy(c + 1, 1 - slot).start()
+
+            m_copy(c, slot).wait()
+            lanes = lax.broadcasted_iota(jnp.int32, (T, KW), 1).astype(F32)
+            for q in range(2 * el):
+                sel[q] = (lanes == mbuf[slot, :, q:q + 1]).astype(F32).astype(BF16)
             for cp in copies:
                 cp.wait()
 
@@ -242,8 +265,10 @@
             def _(i):
                 cols = pl.ds(pl.multiple_of(i * NT, NT), NT)
                 acc = y[:, cols]
-                for p in range(3):
-                    acc = acc + jnp.dot(gbuf[slot, p], rbuf[slot, :, cols], preferred_element_type=F32)
+                for q in range(2 * el):
+                    at = (q % el) * (C2 - KW)
+                    got = jnp.dot(sel[q], rbuf[slot, q // el, at:at + KW, cols], preferred_element_type=F32)
+                    acc = acc + mbuf[slot, :, 2 * el + q:2 * el + q + 1] * got
                 y[:, cols] = acc
 
     @pl.loop(0, D // NT)
@@ -262,11 +287,15 @@
             send(d).wait_send()
 
 
-def _run_exchange(n, axis, C, theirs, u_all, w1, w3, w2, gates, y0):
+def _window(C):
+    return min(256, 2 * C)
+
+
+def _run_exchange(n, axis, C, theirs, u_all, w1, w3, w2, marks, y0):
     T, D = y0.shape
     el, _, FF = w1.shape
     C2, CP = 2 * C, _up(C, 16)
-    KP = gates.shape[-1]
+    KW = _window(C)
     any_spec = pl.BlockSpec(memory_space=pl.ANY)
     dma = pltpu.SemaphoreType.DMA
     rows = n * 2 * C
@@ -286,16 +315,17 @@
             pltpu.VMEM((el, 4 * CP, FF), BF16),
             pltpu.VMEM((4, C2, D), BF16),
             pltpu.VMEM((T, D), F32),
-            pltpu.VMEM((2, 3, T, KP), BF16),
-            pltpu.VMEM((2, KP, D), BF16),
+            pltpu.VMEM((2, T, 4 * el), F32),
+            pltpu.VMEM((2 * el, T, KW), BF16),
+            pltpu.VMEM((2, 2, C2, D), BF16),
             dma((2,)), dma((3,)), dma((4,)), dma((1,)), dma((2,)), dma((2, 2)), dma((n,)), dma((n,)),
         ],
         compiler_params=pltpu.CompilerParams(
             collective_id=0, has_side_effects=True, vmem_limit_bytes=66 * 1000 * 1000),
         cost_estimate=pl.CostEstimate(
-            flops=rows * 6 * D * FF + rows * 8 * T * D, bytes_accessed=rows * D * 8, transcendentals=rows * FF),
+            flops=rows * 6 * D * FF + rows * 6 * T * D, bytes_accessed=rows * D * 8, transcendentals=rows * FF),
         name='exchange',
-    )(theirs, u_all, w1, w3, w2, gates, y0)[0]
+    )(theirs, u_all, w1, w3, w2, marks, y0)[0]
 
 
 def solution(mesh):
@@ -323,15 +353,12 @@
         theirs = lax.all_to_all(place.T, 'expert', 0, 0, tiled=True).reshape(n, el, T)
         theirs = jnp.pad(theirs, ((0, 0), (0, 8 - el), (0, 0)), constant_values=-1)
 
-        per = 2 * el
-        col = jnp.arange(_up(per * C, 128), dtype=jnp.int32)
-        key = jnp.where(has, place + (jnp.arange(E, dtype=jnp.int32) % per) * C, -1)
-        key = key.reshape(T, E // per, per).transpose(1, 0, 2)
-        parts = jnp.stack(_parts(gate)).reshape(3, T, E // per, per).transpose(2, 0, 1, 3)
-        gates = jnp.zeros((), BF16)
-        for k in range(per):
-            hit = key[:, None, :, k, None] == col
-            gates = jnp.where(hit, parts[:, :, :, k, None], gates)
+        src = _peer(n, me, jnp.arange(n, dtype=jnp.int32), False)
+        experts = (src[:, None] * el + jnp.arange(el, dtype=jnp.int32)).reshape(-1)
+        shift = jnp.arange(E, dtype=jnp.int32) % el * (C - (2 * C - _window(C)))
+        row = jnp.where(has, place + shift, -1).astype(F32)
+        marks = jnp.stack([row.T[experts], gate.T[experts]]).reshape(2, n // 2, 2 * el, T)
+        marks = marks.transpose(1, 3, 0, 2).reshape(n // 2, T, 4 * el)
 
         chunks = _attention_chunks(x, ln1, wq, wk, wv, wo, CHUNKS)
         u = _rms(chunks.send(None), ln2)
@@ -342,7 +369,7 @@
         hot_rows = jnp.dot(hot_hit.astype(BF16), u, preferred_element_type=F32).astype(BF16)
         hot_out = _ffn(hot_rows, *hw)
         y0 = _gated([v[None, :] for v in _parts(hot_g)], hot_hit.T, hot_out)
-        return _run_exchange(n, 'expert', C, theirs, u_all, w1, w3, w2, gates, y0)
+        return _run_exchange(n, 'expert', C, theirs, u_all, w1, w3, w2, marks, y0)
 
     tk = ('data', 'expert')
     rep3 = P(None, None, None)

time: 1160 us -> 939 us (0.81)
  the two profiles are of different devices: /device:TPU:97 before, /device:TPU:107 now
where the time goes in v3:
time: 939 us; the launch traced here: 926 us
  Pallas kernels  490 us (52%)
  waiting for transfers between devices  254 us (27%)
  matrix products  87 us (9%)
  local copies, waits for them, and re-layouts  40.4 us (4%)
  other arithmetic  34.6 us (4%)
  between operations  14.1 us (2%)
    pallas_call x1, Pallas kernels, _run_exchange(): pl.pallas_call(functools.partial(_exchange, n, axis), out_shape=(jax.Shap...  490 us
    all_gather x1, waiting for transfers between devices, local(): u_all = lax.all_gather(u, 'expert')  236 us
    unnamed x35, local copies, waits for them, and re-layouts  32.1 us
    dot_general x1, matrix products, _attention_chunks(): out = jnp.einsum('qhk,hkd->qd', o, wo, preferred_element_type=F32)  21.6 us
    sub x1, matrix products, _attention_chunks(): p = jax.nn.softmax(jnp.where(mask[None], s, -jnp.inf), axis=-1).astype(BF16)  19 us
  transfers between devices with their start and end apart: 3, of which 2 were waited for; matrix products, arithmetic and copies ran while one was open for 16% of the time, Pallas kernels for 0%

profile of v3, /device:TPU:107, one launch (start us, length us, event | category | flops | bytes accessed | tf_op | source)
XLA Modules:
  0.0 926.0 jit_solution(4236336124171559477)
XLA Ops:
  6.6 4.7 select_bitcast_fusion
  12.7 5.1 select_bitcast_fusion.1
  21.4 12.3 %copy.33 = bf16[2048,16,128]{0,2,1:T(8,128)(2,1)} copy(bf16[2048,16,128]{2,1,0:T(8,128)(2,1)} %param.20) | data formatting | bytes 16777216 | tf_op args[6]
  33.7 10.4 %fusion.8 = bf16[768,16,128]{2,0,1:T(8,128)(2,1)} fusion(bf16[2048,16,128]{2,1,0:T(8,128)(2,1)} %param.22, bf16[768,2048]{1,0:T(8,128)(2,1)S(1)} %copy-done.3, f32[2048]{0:T(1024)S(1)} %copy-done.15, f32[768]{0:T(1024)S(1)} %add_rsqrt_fusion.1), kind=kOutput, calls=%fused_computation.15 | convolution fusion | flops 6448742400 | bytes 14691328 | tf_op jit(solution)/shard_map/td,dhk->thk/dot_general | solution.py:49
  44.1 9.0 fusion.75
  53.1 12.3 %copy.34 = bf16[2048,16,128]{0,2,1:T(8,128)(2,1)} copy(bf16[2048,16,128]{2,1,0:T(8,128)(2,1)} %param.21) | data formatting | bytes 16777216 | tf_op args[7]
  65.4 9.4 %fusion.73 = f32[768,2048]{0,1:S(1)} fusion(bf16[2048,2048]{0,1:T(8,128)(2,1)} %bitcast.46, bf16[768,2048]{1,0:T(8,128)(2,1)S(1)} %copy-done.3, f32[2048]{0:T(1024)S(1)} %copy-done.15, f32[768]{0:T(1024)S(1)} %add_rsqrt_fusion.1), kind=kOutput, calls=%fused_computation.128 | convolution fusion | flops 6448742400 | bytes 17837056
  74.8 4.0 subtract_convert_fusion.1
  78.8 19.0 %fusion.78 = (f32[16,768]{1,0:T(8,128)S(1)}, f32[16,768,768]{1,2,0:T(8,128)}) fusion(pred[768,768]{0,1:T(8,128)(4,1)} %iota_compare_fusion, bf16[768,16,64]{0,2,1:T(8,128)(2,1)} %get-tuple-element.22, bf16[768,16,64]{0,2,1:T(8,128)(2,1)} %get-tuple-element.23, bf16[768,16,64]{0,2,1:T(8,128)(2,1)} %get-tuple-element.19, ...), kind=kOutput, calls=%fused_computation.130 | convolution fusion | flops 2466251520 | bytes 44679168 | tf_op jit(solution)/shard_map/sub | solution.py:54
  97.8 21.6 %fusion.10 = (f32[768]{0:T(1024)S(1)}, bf16[768,2048]{1,0:T(8,128)(2,1)}) fusion(bf16[16,128,2048]{2,1,0:T(8,128)(2,1)} %param.23, f32[16,768,768]{1,2,0:T(8,128)} %get-tuple-element.33, f32[16,768]{1,0:T(8,128)S(1)} %get-tuple-element.32, bf16[768,16,128]{2,0,1:T(8,128)(2,1)} %fusion.8, bf16[768,2048]{1,0:T(8,128)(2,1)S(1)} %copy-done.3), kind=kOutput, calls=%fused_computation.19 | convolution fusion | flops 8888253440 | bytes 55626752 | tf_op jit(solution)/shard_map/qhk,hkd->qd/dot_general | solution.py:56
  119.4 4.3 fusion.12
  123.8 17.3 %all-reduce.4.cloned.1.call-done = (bf16[2048,1024]{1,0:T(8,128)(2,1)}, bf16[2048,1024]{1,0:T(8,128)(2,1)}, bf16[1024,2048]{1,0:T(8,128)(2,1)}) async-done(((bf16[2048,1024]{1,0:T(8,128)(2,1)}, bf16[2048,1024]{1,0:T(8,128)(2,1)}, bf16[1024,2048]{1,0:T(8,128)(2,1)}), (bf16[2048,1024]{1,0:T(8,128)(2,1)}, bf16[2048,1024]{1,0:T(8,128)(2,1)}, bf16[1024,2048]{1,0:T(8,128)(2,1)})) %all-reduce.4.cloned.1.call-update) | async-done | bytes 12582928 | tf_op jit(solution)/shard_map/psum | solution.py:345
  142.3 6.4 all-to-all-start
  150.9 4.0 copy.42.marks
  154.9 1.5 fusion.32
  156.4 1.9 pad.4.theirs
  158.4 1.4 convolution_convert_fusion
  160.6 1.8 fusion.79
  162.7 2.0 multiply_convert_fusion
  164.7 12.1 %fusion.22 = f32[2304,2048]{1,0:T(8,128)} fusion(bf16[384,1024]{1,0:T(8,128)(2,1)S(1)} %multiply_convert_fusion, bf16[1024,2048]{1,0:T(8,128)(2,1)} %get-tuple-element.13, bf16[768,384]{1,0:T(8,128)(2,1)S(1)} %copy-done.6, bf16[768,384]{1,0:T(8,128)(2,1)S(1)} %copy-done.7, bf16[768,384]{1,0:T(8,128)(2,1)S(1)} %copy-done.5), kind=kOutput, calls=%fused_computation.41 | convolution fusion | flops 5240586240 | bytes 25624576 | tf_op jit(solution)/shard_map/dot_general | solution.py:81
  176.8 11.9 %reduce_sum.49.y0 = f32[768,2048]{1,0:T(8,128)} reduce(f32[3,768,2048]{2,1,0:T(8,128)} %bitcast.43, f32[]{:T(128)} %constant.95.clone.1), dimensions={0}, to_apply=%region_9.10 | reduce | flops 3145728 | bytes 25165828 | tf_op jit(solution)/shard_map/reduce_sum | solution.py:82
  188.7 236.2 %all-gather.3.cloned.1.call-done = bf16[24576,2048]{1,0:T(8,128)(2,1)} async-done(((bf16[768,2048]{1,0:T(8,128)(2,1)}), bf16[24576,2048]{1,0:T(8,128)(2,1)}) %all-gather.3.cloned.1.call-update) | async-done | bytes 100663312 | tf_op jit(solution)/shard_map/all_gather | solution.py:366
  424.9 489.9 %exchange.1 = (bf16[768,2048]{1,0:T(8,128)(2,1)}, bf16[32,272,2048]{2,1,0:T(8,128)(2,1)}, bf16[32,272,2048]{2,1,0:T(8,128)(2,1)}) custom-call(s32[32,8,768]{2,1,0:T(8,128)} %pad.4.theirs, bf16[32,768,2048]{2,1,0:T(8,128)(2,1)} %bitcast.11.u_all, bf16[2,2048,1024]{2,1,0:T(8,128)(2,1)} %w1.1, bf16[2,2048,1024]{2,1,0:T(8,128)(2,1)} %w3.1, ...), custom_call_target="tpu_custom_call" | custom-call | flops 191662915584 | bytes 142606336 | tf_op jit(solution)/shard_map/exchange/pallas_call | solution.py:302
  914.8 4.0 copy.54
  (61 shorter events, 9.5 us)
Async XLA Ops:
  6.5 134.5 %all-reduce.4.cloned.1.call-start = ((), (), s32[]{:S(2)}) async-start(), calls=%async_computation.2 | async-start | bytes 25165824 | tf_op jit(solution)/shard_map/psum | solution.py:345
  6.6 6.2 copy-start.4
  17.8 2.1 copy-start.3
  17.9 407.0 %all-gather.3.cloned.1.call-start = ((), (), s32[]{:S(2)}) async-start(), calls=%async_computation.1 | async-start | bytes 103809024 | tf_op jit(solution)/shard_map/all_gather | solution.py:366
  21.4 12.3 %copy-start.15 = (f32[2048]{0:T(1024)S(1)}, f32[2048]{0:T(1024)}, u32[]{:S(2)}) copy-start(f32[2048]{0:T(1024)} %param.19) | copy-start | bytes 24580
  33.7 10.5 %copy-start.1 = (bf16[2048,16,128]{0,2,1:T(8,128)(2,1)S(1)}, bf16[2048,16,128]{0,2,1:T(8,128)(2,1)}, u32[]{:S(2)}) copy-start(bf16[2048,16,128]{0,2,1:T(8,128)(2,1)} %copy.33) | copy-start | bytes 25165828
  65.3 9.4 %copy-start.2 = (f32[768,2048]{0,1:S(1)}, f32[768,2048]{0,1}, u32[]{:S(2)}) copy-start(f32[768,2048]{0,1} %fusion.75) | copy-start | bytes 18874372
  97.8 21.7 %copy-start.10 = (f32[2048]{0:T(1024)S(1)}, f32[2048]{0:T(1024)}, u32[]{:S(2)}) copy-start(f32[2048]{0:T(1024)} %param.24) | copy-start | bytes 24580
  123.8 17.4 %copy-start.8 = (s32[768,7]{0,1:T(8,128)S(1)}, s32[768,7]{0,1:T(8,128)}, u32[]{:S(2)}) copy-start(s32[768,7]{0,1:T(8,128)} %param.15) | copy-start | bytes 64516
  141.0 8.1 copy-start.9
  142.3 14.1 %all-to-all-start = ((s32[32,2,768]{2,1,0:T(2,128)}), s32[32,2,768]{2,1,0:T(2,128)}, u32[]{:S(2)}, u32[]{:S(2)}) async-start(s32[32,2,768]{2,1,0:T(2,128)} %all_to_all.6), calls=%async_computation | async-start | bytes 393216 | tf_op jit(solution)/shard_map/all_to_all | solution.py:353
  150.9 4.0 copy-start.12
  150.9 4.0 copy-start.11
  150.9 7.4 copy-start
  158.4 2.2 copy-start.14
  160.5 2.2 copy-start.13
  162.7 2.0 copy-start.5
  162.7 2.0 copy-start.6
  162.7 2.0 copy-start.7
Sparse Core Ops, SparseCore 0:
  18.0 123.0 all-reduce.3
  143.1 281.7 all-gather.2

commit v4 on v3

--- a/solution.py
+++ b/solution.py
@@ -69,48 +69,37 @@
     return jnp.dot(z, w2, preferred_element_type=F32).astype(BF16)
 
 
-def _parts(g):
-    hi = lax.reduce_precision(g, 8, 7)
-    mid = lax.reduce_precision(g - hi, 8, 7)
-    low = g - hi - mid
-    return [v.astype(BF16) for v in (hi, mid, low)]
-
-
-def _gated(g_parts, hit, rows):
-    lhs = jnp.concatenate([jnp.where(hit, v, jnp.zeros((), BF16)) for v in g_parts], axis=0)
-    out = jnp.dot(lhs, rows, preferred_element_type=F32)
-    return jnp.sum(out.reshape(len(g_parts), -1, out.shape[-1]), axis=0)
-
-
 def _up(v, m):
     return (v + m - 1) // m * m
 
 
-ORDER4 = ((0, 1), (2, 0), (1, 3), (0, 2), (0, 0), (3, 0), (1, 1), (2, 1),
-          (0, 3), (3, 3), (3, 1), (1, 0), (2, 3), (3, 2), (2, 2), (1, 2))
+ORDER4 = (4, 14, 28, 13, 12, 20, 1, 19, 3, 8, 24, 16, 17, 2, 21, 5,
+          29, 15, 31, 9, 23, 7, 0, 18, 25, 27, 11, 6, 10, 22, 26, 30)
 
 
 def _side(n):
     return math.isqrt(n // 2)
 
 
-def _offset(side, o):
-    order = ORDER4 if side == 4 else tuple((i % side, i // side) for i in range(side * side))
+def _offset(n, k):
+    side = _side(n)
+    order = ORDER4 if side == 4 else tuple(i % side + i // side % side * 4 + i // (n // 2) * 16 for i in range(n))
+    bit0, bit1 = lax.rem(lax.div(k, 8), 2), lax.div(k, 16)
+    q = lax.rem(k, 8)
+    power = (1 + 3 * lax.rem(q, 2)) * (1 + 15 * lax.rem(lax.div(q, 2), 2)) * (1 + 255 * lax.div(q, 4))
 
     def digit(vals):
-        lo, hi = (sum(v * 4 ** i for i, v in enumerate(vals[h * 8:h * 8 + 8])) for h in range(2))
-        q = lax.rem(o, 8)
-        power = ((1 + 3 * lax.rem(q, 2)) * (1 + 15 * lax.rem(lax.div(q, 2), 2)) * (1 + 255 * lax.div(q, 4)))
-        return lax.rem(lax.div(lo + lax.div(o, 8) * (hi - lo), power), 4)
-
-    return digit([v[0] for v in order]), digit([v[1] for v in order])
+        a, b, c, d = (sum(v * 4 ** i for i, v in enumerate(vals[h * 8:h * 8 + 8])) for h in range(4))
+        pack = (a * (1 - bit0) + b * bit0) * (1 - bit1) + (c * (1 - bit0) + d * bit0) * bit1
+        return lax.rem(lax.div(pack, power), 4)
+
+    return digit([v % 4 for v in order]), digit([v // 4 % 4 for v in order]), digit([v // 16 for v in order])
 
 
 def _peer(n, me, k, sending):
     side = _side(n)
     core, chip = lax.rem(me, 2), lax.div(me, 2)
-    other = lax.rem(k, 2)
-    dx, dy = _offset(side, lax.div(k, 2))
+    dx, dy, other = _offset(n, k)
     their = lax.rem(core + other, 2)
     sign = 1 - 2 * core if sending else 2 * their - 1
     px = lax.rem(lax.rem(chip, side) + sign * dx + side, side)
@@ -165,10 +154,10 @@
 
     pl.semaphore_wait(barrier, n - 1)
 
-    @pl.loop(0, n // 4)
-    def _(b):
-        for j in range(4):
-            k = b * 4 + j
+    def step(first, batch):
+        m = batch * CP
+        for j in range(batch):
+            k = first + j
             slot = j % 2
             u_copy(k, slot).wait()
             where = theirs[dest(k)]
@@ -186,7 +175,7 @@
             def _():
                 u_copy(k + 2, slot).start()
 
-        @pl.when(b == 0)
+        @pl.when(first == 0)
         def _():
             for cp in weights:
                 cp.wait()
@@ -195,21 +184,21 @@
             @pl.loop(0, FF // FT)
             def _(i):
                 cols = pl.ds(pl.multiple_of(i * FT, FT), FT)
-                h1 = jnp.dot(xin[l], v1[l, :, cols], preferred_element_type=F32)
-                h3 = jnp.dot(xin[l], v3[l, :, cols], preferred_element_type=F32)
-                z[l, :, cols] = (h1 * jax.nn.sigmoid(h1) * h3).astype(BF16)
+                h1 = jnp.dot(xin[l, :m], v1[l, :, cols], preferred_element_type=F32)
+                h3 = jnp.dot(xin[l, :m], v3[l, :, cols], preferred_element_type=F32)
+                z[l, :m, cols] = (h1 * jax.nn.sigmoid(h1) * h3).astype(BF16)
 
         @pl.loop(0, D // NT)
         def _(i):
             cols = pl.ds(pl.multiple_of(i * NT, NT), NT)
-            o0 = jnp.dot(z[0], v2[0, :, cols], preferred_element_type=F32)
-            o1 = jnp.dot(z[1], v2[1, :, cols], preferred_element_type=F32)
-            for j in range(4):
+            o0 = jnp.dot(z[0, :m], v2[0, :, cols], preferred_element_type=F32)
+            o1 = jnp.dot(z[1, :m], v2[1, :, cols], preferred_element_type=F32)
+            for j in range(batch):
                 both = jnp.concatenate([o0[j * CP:j * CP + C], o1[j * CP:j * CP + C]], axis=0)
                 out[j, :, cols] = both.astype(BF16)
 
-        for j in range(4):
-            d = dest(b * 4 + j)
+        for j in range(batch):
+            d = dest(first + j)
 
             @pl.when(d != me)
             def _():
@@ -219,8 +208,8 @@
             def _():
                 pltpu.make_async_copy(out.at[j], recv.at[me], o_sem.at[j]).start()
 
-        for j in range(4):
-            d = dest(b * 4 + j)
+        for j in range(batch):
+            d = dest(first + j)
 
             @pl.when(d != me)
             def _():
@@ -230,6 +219,14 @@
             @pl.when(d == me)
             def _():
                 pltpu.make_async_copy(out.at[j], recv.at[me], o_sem.at[j]).wait()
+
+    @pl.loop(0, 2)
+    def _(b):
+        step(b * 2, 2)
+
+    @pl.loop(1, n // 4)
+    def _(b):
+        step(b * 4, 4)
 
     y_copy.wait()
 
@@ -368,7 +365,8 @@
         hot_hit = hot_tok[:, None] == jnp.arange(T, dtype=jnp.int32)
         hot_rows = jnp.dot(hot_hit.astype(BF16), u, preferred_element_type=F32).astype(BF16)
         hot_out = _ffn(hot_rows, *hw)
-        y0 = _gated([v[None, :] for v in _parts(hot_g)], hot_hit.T, hot_out)
+        token_g = jnp.sum(jnp.where(hot_hit, hot_g[:, None], 0.0), axis=0)
+        y0 = token_g[:, None] * jnp.dot(hot_hit.T.astype(BF16), hot_out, preferred_element_type=F32)
         return _run_exchange(n, 'expert', C, theirs, u_all, w1, w3, w2, marks, y0)
 
     tk = ('data', 'expert')

time: 939 us -> 961 us (1.023)
  the two profiles are of different devices: /device:TPU:107 before, /device:TPU:97 now
where the time goes in v4:
time: 961 us; the launch traced here: 952 us
  Pallas kernels  512 us (53%)
  waiting for transfers between devices  276 us (29%)
  matrix products  83 us (9%)
  local copies, waits for them, and re-layouts  40.5 us (4%)
  other arithmetic  21.4 us (2%)
  between operations  14.1 us (1%)
    pallas_call x1, Pallas kernels, _run_exchange(): pl.pallas_call(functools.partial(_exchange, n, axis), out_shape=(jax.Shap...  512 us
    all_gather x1, waiting for transfers between devices, local(): u_all = lax.all_gather(u, 'expert')  255 us
    unnamed x29, local copies, waits for them, and re-layouts  32.2 us
    dot_general x1, matrix products, _attention_chunks(): out = jnp.einsum('qhk,hkd->qd', o, wo, preferred_element_type=F32)  21.5 us
    psum x1, waiting for transfers between devices, local(): lax.psum(jnp.where(own, w[lh], jnp.zeros((), BF16)), 'expert')  19.8 us
  transfers between devices with their start and end apart: 3, of which 3 were waited for; matrix products, arithmetic and copies ran while one was open for 13% of the time, Pallas kernels for 0%

profile of v4, /device:TPU:97, one launch (start us, length us, event | category | flops | bytes accessed | tf_op | source)
XLA Modules:
  0.0 951.7 jit_solution(6702822657768214742)
XLA Ops:
  6.6 4.7 select_bitcast_fusion
  11.3 1.4 copy-done.4
  12.7 5.1 select_bitcast_fusion.1
  21.4 12.4 %copy.33 = bf16[2048,16,128]{0,2,1:T(8,128)(2,1)} copy(bf16[2048,16,128]{2,1,0:T(8,128)(2,1)} %param.20) | data formatting | bytes 16777216 | tf_op args[6]
  33.7 10.4 %fusion.8 = bf16[768,16,128]{2,0,1:T(8,128)(2,1)} fusion(bf16[2048,16,128]{2,1,0:T(8,128)(2,1)} %param.22, bf16[768,2048]{1,0:T(8,128)(2,1)S(1)} %copy-done.3, f32[2048]{0:T(1024)S(1)} %copy-done.12, f32[768]{0:T(1024)S(1)} %add_rsqrt_fusion.1), kind=kOutput, calls=%fused_computation.15 | convolution fusion | flops 6448742400 | bytes 14691328 | tf_op jit(solution)/shard_map/td,dhk->thk/dot_general | solution.py:49
  44.2 9.0 fusion.79
  53.2 12.3 %copy.34 = bf16[2048,16,128]{0,2,1:T(8,128)(2,1)} copy(bf16[2048,16,128]{2,1,0:T(8,128)(2,1)} %param.21) | data formatting | bytes 16777216 | tf_op args[7]
  65.5 9.4 fusion.77
  74.9 3.9 subtract_convert_fusion.1
  78.9 19.0 %fusion.82 = (f32[16,768]{1,0:T(8,128)S(1)}, f32[16,768,768]{1,2,0:T(8,128)}) fusion(pred[768,768]{0,1:T(8,128)(4,1)} %iota_compare_fusion, bf16[768,16,64]{0,2,1:T(8,128)(2,1)} %get-tuple-element.22, bf16[768,16,64]{0,2,1:T(8,128)(2,1)} %get-tuple-element.23, bf16[768,16,64]{0,2,1:T(8,128)(2,1)} %get-tuple-element.19, ...), kind=kOutput, calls=%fused_computation.133 | convolution fusion | flops 2466251520 | bytes 44679168 | tf_op jit(solution)/shard_map/sub | solution.py:54
  97.9 21.5 %fusion.10 = (f32[768]{0:T(1024)S(1)}, bf16[768,2048]{1,0:T(8,128)(2,1)}) fusion(bf16[16,128,2048]{2,1,0:T(8,128)(2,1)} %param.23, f32[16,768,768]{1,2,0:T(8,128)} %get-tuple-element.27, f32[16,768]{1,0:T(8,128)S(1)} %get-tuple-element.26, bf16[768,16,128]{2,0,1:T(8,128)(2,1)} %fusion.8, bf16[768,2048]{1,0:T(8,128)(2,1)S(1)} %copy-done.3), kind=kOutput, calls=%fused_computation.19 | convolution fusion | flops 8888253440 | bytes 55626752 | tf_op jit(solution)/shard_map/qhk,hkd->qd/dot_general | solution.py:56
  119.4 4.3 fusion.12
  123.7 19.8 %all-reduce.4.cloned.1.call-done = (bf16[2048,1024]{1,0:T(8,128)(2,1)}, bf16[2048,1024]{1,0:T(8,128)(2,1)}, bf16[1024,2048]{1,0:T(8,128)(2,1)}) async-done(((bf16[2048,1024]{1,0:T(8,128)(2,1)}, bf16[2048,1024]{1,0:T(8,128)(2,1)}, bf16[1024,2048]{1,0:T(8,128)(2,1)}), (bf16[2048,1024]{1,0:T(8,128)(2,1)}, bf16[2048,1024]{1,0:T(8,128)(2,1)}, bf16[1024,2048]{1,0:T(8,128)(2,1)})) %all-reduce.4.cloned.1.call-update) | async-done | bytes 12582928 | tf_op jit(solution)/shard_map/psum | solution.py:342
  144.9 5.4 all-to-all-start
  152.4 4.0 copy.42.marks
  156.6 1.1 all-to-all-done
  157.7 1.9 pad.4.theirs
  159.6 1.4 convolution_convert_fusion
  161.8 1.8 fusion.83
  164.0 1.9 multiply_convert_fusion
  165.9 8.2 convolution_multiply_fusion.y0
  174.1 254.6 %all-gather.3.cloned.1.call-done = bf16[24576,2048]{1,0:T(8,128)(2,1)} async-done(((bf16[768,2048]{1,0:T(8,128)(2,1)}), bf16[24576,2048]{1,0:T(8,128)(2,1)}) %all-gather.3.cloned.1.call-update) | async-done | bytes 100663312 | tf_op jit(solution)/shard_map/all_gather | solution.py:363
  428.7 511.7 %exchange.1 = (bf16[768,2048]{1,0:T(8,128)(2,1)}, bf16[32,272,2048]{2,1,0:T(8,128)(2,1)}, bf16[32,272,2048]{2,1,0:T(8,128)(2,1)}) custom-call(s32[32,8,768]{2,1,0:T(8,128)} %pad.4.theirs, bf16[32,768,2048]{2,1,0:T(8,128)(2,1)} %bitcast.11.u_all, bf16[2,2048,1024]{2,1,0:T(8,128)(2,1)} %w1.1, bf16[2,2048,1024]{2,1,0:T(8,128)(2,1)} %w3.1, ...), custom_call_target="tpu_custom_call" | custom-call | flops 191662915584 | bytes 142606336 | tf_op jit(solution)/shard_map/exchange/pallas_call | solution.py:299
  940.5 4.0 copy.54
  (53 shorter events, 8.3 us)
Async XLA Ops:
  6.5 137.0 %all-reduce.4.cloned.1.call-start = ((), (), s32[]{:S(2)}) async-start(), calls=%async_computation.2 | async-start | bytes 25165824 | tf_op jit(solution)/shard_map/psum | solution.py:342
  6.6 6.2 copy-start.4
  17.8 2.1 copy-start.3
  17.9 410.9 %all-gather.3.cloned.1.call-start = ((), (), s32[]{:S(2)}) async-start(), calls=%async_computation.1 | async-start | bytes 103809024 | tf_op jit(solution)/shard_map/all_gather | solution.py:363
  21.4 12.4 %copy-start.12 = (f32[2048]{0:T(1024)S(1)}, f32[2048]{0:T(1024)}, u32[]{:S(2)}) copy-start(f32[2048]{0:T(1024)} %param.19) | copy-start | bytes 24580
  33.7 10.5 %copy-start.1 = (bf16[2048,16,128]{0,2,1:T(8,128)(2,1)S(1)}, bf16[2048,16,128]{0,2,1:T(8,128)(2,1)}, u32[]{:S(2)}) copy-start(bf16[2048,16,128]{0,2,1:T(8,128)(2,1)} %copy.33) | copy-start | bytes 25165828
  65.5 9.4 copy-start.2
  97.9 21.5 %copy-start.7 = (f32[2048]{0:T(1024)S(1)}, f32[2048]{0:T(1024)}, u32[]{:S(2)}) copy-start(f32[2048]{0:T(1024)} %param.24) | copy-start | bytes 24580
  123.7 19.9 %copy-start.5 = (s32[768,7]{0,1:T(8,128)S(1)}, s32[768,7]{0,1:T(8,128)}, u32[]{:S(2)}) copy-start(s32[768,7]{0,1:T(8,128)} %param.15) | copy-start | bytes 64516
  143.5 7.1 copy-start.6
  144.9 12.8 %all-to-all-start = ((s32[32,2,768]{2,1,0:T(2,128)}), s32[32,2,768]{2,1,0:T(2,128)}, u32[]{:S(2)}, u32[]{:S(2)}) async-start(s32[32,2,768]{2,1,0:T(2,128)} %all_to_all.6), calls=%async_computation | async-start | bytes 393216 | tf_op jit(solution)/shard_map/all_to_all | solution.py:350
  152.4 4.0 copy-start.8
  152.4 4.0 copy-start.9
  152.4 7.2 copy-start
  159.6 2.2 copy-start.11
  161.8 2.2 copy-start.10
Sparse Core Ops, SparseCore 0:
  18.0 125.5 all-reduce.3
  145.6 283.0 all-gather.2
